TPU v7x, 32 devices: a whole 2x2x4 slice. The times are simulated.
32 devices in a mesh: groups: 2 (over x), strip: 16 (over z, y, core).
Axes of the slice: x: 2, y: 2, z: 4, core: 2. Of those that a mesh axis runs over, the one named last changes fastest.
Arguments:
- incoming_wave: float32 [8, 2, 256, 1024], P('groups', None, 'strip'), parts along dimension 0, may hold values from -64 to 64
- speed_class_map: int32 [4, 256, 1024], P('groups', 'strip'), parts along dimension 0, may hold values from 0 to 15
- spectral_entry_index: int32 [8, 4], P('groups'), parts along dimension 0, may hold values from 0 to 15
- filter_weights: float32 [16, 16, 2, 13], replicated, may hold values from -1.6 to 1.6
- scaled_pulsations: float32 [16], replicated, may hold values from 1 to 6
- inverse_speed_classes: float32 [16], replicated, may hold values from 0.3 to 1.5
Outputs:
- image: float32 [4, 256, 1024], P('groups', 'strip'), parts along dimension 0
- handed: float32 [8, 2, 256, 1024], P('groups', None, 'strip'), parts along dimension 0
There are 2 independent parts, one for each index of `groups`. A program takes and returns all parts, laid end to end along the dimension named above; an argument that names none is the same for every part. Nothing has to cross between parts.
All inputs are finite; a program needn't handle non-finite values.
Results may differ from a plain program's by a relative error of at most 0.0003.
Values sent between devices are 32-bit elements; how exact they have to be, the bound alone decides.
A program may use at most 128 MiB of HBM per device.

v0:
```python
import functools
import jax
import jax.numpy as jnp
from jax import lax
from jax.experimental import pallas as pl
from jax.experimental.pallas import tpu as pltpu
from jax.sharding import PartitionSpec as P

SECTIONS = 4
LEVELS = 2
ORDER = 12
NFREQ = 4
NBIN = 16
NW = 16


def extended_2(shard, sides, width):
    for axis, dim in sides:
        devices, length = (lax.axis_size(axis), shard.shape[dim])
        up = [(i, (i + 1) % devices) for i in range(devices)]
        down = [(j, i) for i, j in up]
        last = lax.slice_in_dim(shard, length - width, length, axis=dim)
        initial = lax.slice_in_dim(shard, 0, width, axis=dim)
        before = lax.ppermute(last, axis, up)
        after = lax.ppermute(initial, axis, down)
        shard = jnp.concatenate([before, shard, after], axis=dim)
    return shard


def from_behind(shard, axis, by):
    devices = lax.axis_size(axis)
    return lax.ppermute(shard, axis, [(i, (i + by) % devices) for i in range(devices)])


def stencil_padded(padded):
    vertical = padded[:, :, :-2, :] + padded[:, :, 2:, :]
    middle = padded[:, :, 1:-1, :]
    return (
        -0.5 * middle[..., 1:-1]
        + 0.25 * (vertical[..., 1:-1] + middle[..., :-2] + middle[..., 2:])
        + 0.125 * (vertical[..., :-2] + vertical[..., 2:])
    )


def complex_times(coeff, field):
    real_part = coeff[:, 0] * field[:, 0] - coeff[:, 1] * field[:, 1]
    imag_part = coeff[:, 0] * field[:, 1] + coeff[:, 1] * field[:, 0]
    return jnp.stack([real_part, imag_part], axis=1)


def shards(
    incoming_wave,
    speed_class_map,
    spectral_entry_index,
    filter_weights,
    scaled_pulsations,
    inverse_speed_classes,
):
    highest = lax.Precision.HIGHEST
    summed_along = incoming_wave.shape[2]
    summed_across = incoming_wave.shape[3]
    strip_count = lax.axis_size("strip")
    lateral_count = strip_count // SECTIONS
    position = (lax.axis_index("strip") - lateral_count // 2) % strip_count
    vertical_slab = position // lateral_count
    lateral_place = position % lateral_count
    section_rows = summed_along * lateral_count
    section_cells = section_rows * summed_across
    margin = ORDER
    extended_rows = summed_along + 2 * margin
    lateral_rows = (
        lateral_place * summed_along - margin + jnp.arange(extended_rows, dtype=jnp.int32)
    )
    inside = ((lateral_rows >= 0) & (lateral_rows < section_rows)).astype(jnp.float32)[
        None, None, :, None
    ]

    def mcclellan_step(field):
        padded = jnp.pad(field, ((0, 0), (0, 0), (1, 1), (0, 0)))
        padded = jnp.pad(padded, ((0, 0), (0, 0), (0, 0), (1, 1)))
        result = stencil_padded(padded)
        result = result * inside
        return result

    def interior(field):
        return field[:, :, margin : margin + summed_along, :]

    def image_downward(field, batch_index):
        freq_row = lax.dynamic_index_in_dim(spectral_entry_index, batch_index, 0, keepdims=False)
        freq_select = (freq_row[:, None] == jnp.arange(NW, dtype=jnp.int32)[None, :]).astype(
            jnp.float32
        )
        freq_coeffs = jnp.einsum("fw,wbck->fbck", freq_select, filter_weights, precision=highest)
        freq_omega = jnp.dot(freq_select, scaled_pulsations, precision=highest)
        wavefield = field
        raws = []
        for level in range(LEVELS):
            cells = speed_class_map[level].reshape(-1)
            bin_onehot = (cells[None, :] == jnp.arange(NBIN, dtype=jnp.int32)[:, None]).astype(
                jnp.float32
            )
            cell_slowness = jnp.dot(inverse_speed_classes, bin_onehot, precision=highest).reshape(
                summed_along, summed_across
            )
            table = jnp.einsum("fbck,bn->kfcn", freq_coeffs, bin_onehot, precision=highest).reshape(
                ORDER + 1, NFREQ, 2, summed_along, summed_across
            )
            extended = extended_2(wavefield, (("strip", 2),), ORDER) * inside
            previous = extended
            current = mcclellan_step(extended)
            accumulated = complex_times(table[0], interior(previous)) + complex_times(
                table[1], interior(current)
            )

            def recursion_step(order_index, state_tuple):
                before, present, running = state_tuple
                following = 2.0 * mcclellan_step(present) - before
                coeff = lax.dynamic_index_in_dim(table, order_index, 0, keepdims=False)
                running = running + complex_times(coeff, interior(following))
                return (present, following, running)

            previous, current, accumulated = lax.fori_loop(
                2, ORDER + 1, recursion_step, (previous, current, accumulated)
            )
            phase_angle = freq_omega[:, None, None] * cell_slowness[None]
            cosine = jnp.cos(phase_angle)
            sine_part = jnp.sin(phase_angle)
            real_part = accumulated[:, 0] * cosine - accumulated[:, 1] * sine_part
            imag_part = accumulated[:, 0] * sine_part + accumulated[:, 1] * cosine
            wavefield = jnp.stack([real_part, imag_part], axis=1)
            raws.append(jnp.sum(real_part, axis=0))
        return (wavefield, raws)

    above_floor_lines, above_unscaled_waves = image_downward(incoming_wave, vertical_slab)
    arriving = from_behind(above_floor_lines, "strip", lateral_count)
    second_bottom, second_raws = image_downward(arriving, jnp.maximum(vertical_slab - 1, 0))
    handed = jnp.where(vertical_slab == 0, above_floor_lines, second_bottom)
    first_section = (vertical_slab > 0).astype(jnp.float32)
    totals = [
        above_unscaled_waves[level] + first_section * second_raws[level] for level in range(LEVELS)
    ]
    selector = (jnp.arange(SECTIONS, dtype=jnp.int32) == vertical_slab).astype(jnp.float32)
    images = []
    for level in range(LEVELS):
        raw_image = totals[level]
        spread = lax.psum(selector * jnp.sum(raw_image * raw_image), "strip")
        mean_square = jnp.sum(spread * selector) / section_cells
        images.append(raw_image / jnp.sqrt(mean_square + 1e-06))
    return (jnp.stack(images, axis=0), handed)


SUB = 8
LANES = 128
PAD = 5
UNROLL = 8
TOGETHER = 4
MESH = pl.DeviceIdType.MESH


def at_row(row):
    return pl.ds(pl.multiple_of(row * SUB, SUB), SUB)


def kernel(
    strip_count,
    entry_ref,
    wave_ref,
    map_ref,
    table_ref,
    image_ref,
    handed_ref,
    starts,
    work,
    bottom,
    last,
    last_in,
    wave_out,
    map_out,
    map_all,
    raw,
    raw_in,
    sum_own,
    sum_in,
    swap_sems,
    halo_sems,
    hand_sems,
    fin_sems,
    raw_sems,
    sum_sems,
):
    nfh = wave_ref.shape[0] // 2
    length = wave_ref.shape[2]
    rows = 2 * length
    blocks = wave_ref.shape[3] // LANES
    lateral = strip_count // SECTIONS
    shift = lateral // 2
    pairs = lateral // 2
    margin = ORDER
    first = PAD + margin
    me = lax.axis_index("strip")
    position = lax.rem(me + strip_count - shift, strip_count)
    section = position // lateral
    place = lax.rem(position, lateral)
    pair = place // 2
    half = lax.rem(place, 2)
    up = jnp.where(pair > 0, 1, 0)
    down = jnp.where(pair < pairs - 1, 1, 0)
    has_up = pair > 0
    has_down = pair < pairs - 1
    has_before = section > 0
    has_after = section < SECTIONS - 1
    other = 1 - half

    def device(pos):
        return {"strip": lax.rem(pos + shift + strip_count, strip_count)}

    partner = device(position + 1 - 2 * half)
    upper = device(position - 2)
    lower = device(position + 2)
    deeper = device(position + lateral)
    shallower = device(position + strip_count - lateral)

    def remote(src, dst, sems, index, target):
        return pltpu.make_async_remote_copy(
            src_ref=src,
            dst_ref=dst,
            send_sem=sems.at[(0,) + index],
            recv_sem=sems.at[(1,) + index],
            device_id=target,
            device_id_type=MESH,
        )

    def span(row, count):
        return pl.ds(pl.multiple_of(row * SUB, SUB), count * SUB)

    zero = jnp.zeros((SUB, LANES), jnp.float32)
    for edge in (first - 1, first + rows):
        for f in range(nfh):
            for c in range(2):
                for s in range(2 * LEVELS):
                    starts[s, f, c, at_row(edge), :] = zero
        for c in range(2):
            for k in range(ORDER):
                work[k, c, at_row(edge), :] = zero

    barrier = pltpu.get_barrier_semaphore()
    for d in range(1, lateral):
        mate = device(section * lateral + lax.rem(place + d, lateral))
        pl.semaphore_signal(barrier, inc=1, device_id=mate, device_id_type=MESH)
    for target in (deeper, shallower):
        pl.semaphore_signal(barrier, inc=1, device_id=target, device_id_type=MESH)

    def rearrange(load, store):
        for g in range(length // SUB):
            for j in range(blocks):
                store(g, j, load(g, j))

    def strided(row, g, j):
        return pl.ds((row + g * SUB) * SUB + j, SUB, stride=SUB)

    own_row = half * length
    swaps = []
    for f in range(nfh):
        for c in range(2):
            rearrange(
                lambda g, j: wave_ref[other * nfh + f, c, pl.ds(g * SUB, SUB), pl.ds(j * LANES, LANES)],
                lambda g, j, x: pltpu_store(wave_out.at[f, c], strided(0, g, j), x),
            )
        if f == 0:
            pl.semaphore_wait(barrier, lateral + 1)
        copy = remote(
            wave_out.at[f],
            starts.at[0, f, :, span(first + own_row, length), :],
            swap_sems,
            (f,),
            partner,
        )
        copy.start()
        swaps.append(copy)
    for l in range(LEVELS):
        rearrange(
            lambda g, j: map_ref[l, pl.ds(g * SUB, SUB), pl.ds(j * LANES, LANES)],
            lambda g, j, x: pltpu_store(map_out.at[l], strided(0, g, j), x),
        )
    copy = remote(
        map_out, map_all.at[:, span(own_row, length), :], swap_sems, (nfh,), partner
    )
    copy.start()
    swaps.append(copy)
    for f in range(nfh):
        for c in range(2):
            rearrange(
                lambda g, j: wave_ref[half * nfh + f, c, pl.ds(g * SUB, SUB), pl.ds(j * LANES, LANES)],
                lambda g, j, x: pltpu_store(
                    starts.at[0, f, c], strided(first + own_row, g, j), x
                ),
            )
    for l in range(LEVELS):
        rearrange(
            lambda g, j: map_ref[l, pl.ds(g * SUB, SUB), pl.ds(j * LANES, LANES)],
            lambda g, j, x: pltpu_store(map_all.at[l], strided(own_row, g, j), x),
        )

    def halo_up(stage, f):
        ref = starts.at[stage, f]
        return remote(
            ref.at[:, span(first, margin), :],
            ref.at[:, span(first + rows, margin), :],
            halo_sems,
            (stage, f, 0),
            upper,
        )

    def halo_down(stage, f):
        ref = starts.at[stage, f]
        return remote(
            ref.at[:, span(first + rows - margin, margin), :],
            ref.at[:, span(first - margin, margin), :],
            halo_sems,
            (stage, f, 1),
            lower,
        )

    def send_halo(stage, f):
        pl.when(has_up)(lambda: halo_up(stage, f).start())
        pl.when(has_down)(lambda: halo_down(stage, f).start())

    def wait_halo(stage, f):
        pl.when(has_down)(lambda: halo_up(stage, f).wait_recv())
        pl.when(has_up)(lambda: halo_down(stage, f).wait_recv())

    def hand_parts(f):
        parts = ((0, margin), (rows - margin, margin), (margin, rows - 2 * margin))
        return [
            remote(
                bottom.at[f, :, span(row, count), :],
                starts.at[LEVELS, f, :, span(first + row, count), :],
                hand_sems,
                (f, n),
                deeper,
            )
            for n, (row, count) in enumerate(parts)
        ]

    lane = lax.broadcasted_iota(jnp.int32, (SUB, LANES), 1)
    sub = lax.broadcasted_iota(jnp.int32, (SUB, LANES), 0)
    at_first = lane == 0
    at_last = lane == LANES - 1
    keep_first = sub > 0
    keep_last = sub < SUB - 1

    def across(u):
        right = pltpu.roll(u, 1, 1)
        right_fix = jnp.where(keep_first, pltpu.roll(right, 1, 0), 0.0)
        left = pltpu.roll(u, LANES - 1, 1)
        left_fix = jnp.where(keep_last, pltpu.roll(left, SUB - 1, 0), 0.0)
        return jnp.where(at_first, right_fix, right) + jnp.where(at_last, left_fix, left)

    def reach(k):
        return ((margin - k + UNROLL - 1) // UNROLL) * UNROLL

    def apply(k, present, before, target):
        extra = reach(k)
        low = first - up * extra
        count = (rows + (up + down) * extra) // UNROLL

        def block(i, carry):
            base = low + i * UNROLL
            v = [
                [present[c, at_row(base - 1 + n), :] for n in range(UNROLL + 2)]
                for c in range(2)
            ]
            old = None
            if before is not None:
                old = [
                    [before[c, at_row(base + n), :] for n in range(UNROLL)] for c in range(2)
                ]
            values = []
            for c in range(2):
                q = [v[c][n] + v[c][n + 1] for n in range(UNROLL + 1)]
                for n in range(UNROLL):
                    u = q[n] + q[n + 1]
                    w = across(u) + (u + u)
                    centre = v[c][n + 1]
                    if old is None:
                        value = 0.125 * w - centre
                    else:
                        value = 0.25 * w - (centre + centre + old[c][n])
                    values.append(value)
            for c in range(2):
                for n in range(UNROLL):
                    target[c, at_row(base + n), :] = values[c * UNROLL + n]
            return carry

        lax.fori_loop(0, count, block, 0)

    def unit(tick, level, f, meanwhile=None):
        stage = tick * LEVELS + level
        start = starts.at[stage, f]
        apply(1, start, None, work.at[0])
        apply(2, work.at[0], start, work.at[1])

        def step(k, carry):
            apply(k, work.at[k - 2], work.at[k - 3], work.at[k - 1])
            return carry

        lax.fori_loop(3, ORDER + 1, step, 0)
        if meanwhile is not None:
            meanwhile()
        batch = section if tick == 0 else jnp.maximum(section - 1, 0)
        entry = entry_ref[batch, half * nfh + f]

        def combine(i, carry):
            spots = [TOGETHER * i + n for n in range(TOGETHER)]
            bins = [map_all[level, at_row(r), :] for r in spots]
            real = [None] * TOGETHER
            imag = [None] * TOGETHER
            for n, r in enumerate(spots):
                for k in range(ORDER + 1):
                    cr, ci = (
                        jnp.take_along_axis(
                            jnp.broadcast_to(
                                table_ref[entry, pl.ds(2 * k + c, 1), :], (SUB, LANES)
                            ),
                            bins[n],
                            axis=1,
                            mode="promise_in_bounds",
                        )
                        for c in range(2)
                    )
                    source = start if k == 0 else work.at[k - 1]
                    tr = source[0, at_row(first + r), :]
                    ti = source[1, at_row(first + r), :]
                    re = cr * tr - ci * ti
                    im = cr * ti + ci * tr
                    real[n] = re if k == 0 else real[n] + re
                    imag[n] = im if k == 0 else imag[n] + im
            for n, r in enumerate(spots):
                re, im = real[n], imag[n]
                if tick == 0 and f == 0:
                    raw[level, at_row(r), :] = re
                else:
                    part = re if tick == 0 else jnp.where(has_before, re, 0.0)
                    raw[level, at_row(r), :] = raw[level, at_row(r), :] + part
                for c, value in enumerate((re, im)):
                    if level < LEVELS - 1:
                        starts[stage + 1, f, c, at_row(first + r), :] = value
                    elif tick == 0:
                        bottom[f, c, at_row(r), :] = value
                    else:
                        last[f, c, at_row(r), :] = jnp.where(
                            has_before, value, bottom[f, c, at_row(r), :]
                        )
            return carry

        lax.fori_loop(0, rows // TOGETHER, combine, 0)

    def finish_wave(f):
        return remote(
            last.at[f, :, span(other * length, length), :],
            last_in.at[f],
            fin_sems,
            (f,),
            partner,
        )

    def finish_raw(l):
        return remote(
            raw.at[l, span(other * length, length), :], raw_in.at[l], raw_sems, (l,), partner
        )

    for f in range(nfh):
        swaps[f].wait_recv()
        send_halo(0, f)
    swaps[nfh].wait_recv()
    for level in range(LEVELS):
        for f in range(nfh):
            wait_halo(level, f)
            unit(0, level, f)
            if level < LEVELS - 1:
                send_halo(level + 1, f)
            else:

                @pl.when(has_after)
                def _():
                    for copy in hand_parts(f):
                        copy.start()

    def forward(f):
        @pl.when(has_before)
        def _():
            high, low, mid = hand_parts(f)
            high.wait_recv()
            pl.when(has_up)(lambda: halo_up(LEVELS, f).start())
            low.wait_recv()
            pl.when(has_down)(lambda: halo_down(LEVELS, f).start())
            mid.wait_recv()

    def skip_or(fn):
        pl.when(has_before)(fn)

    forward(0)
    for level in range(LEVELS):
        for f in range(nfh):

            @pl.when(has_before)
            def _():
                wait_halo(LEVELS + level, f)

            later = f + 1 if level == 0 and f + 1 < nfh else None
            unit(1, level, f, None if later is None else lambda: forward(later))
            if level < LEVELS - 1:

                @pl.when(has_before)
                def _():
                    send_halo(LEVELS + level + 1, f)

            else:
                finish_wave(f).start()
        finish_raw(level).start()

    for l in range(LEVELS):
        finish_raw(l).wait_recv()

        def merge(i, carry):
            value = raw[l, at_row(own_row + i), :] + raw_in[l, at_row(i), :]
            raw_in[l, at_row(i), :] = value
            return carry + value * value

        sum_own[pl.ds(l * SUB, SUB), :] = lax.fori_loop(0, length, merge, zero)
    for d in range(1, lateral):
        mate = device(section * lateral + lax.rem(place + d, lateral))
        remote(sum_own, sum_in.at[d], sum_sems, (d,), mate).start()

    for f in range(nfh):
        for c in range(2):
            rearrange(
                lambda g, j: last[f, c, strided(own_row, g, j), :],
                lambda g, j, x: out_store(handed_ref, half * nfh + f, c, g, j, x),
            )
    for f in range(nfh):
        finish_wave(f).wait_recv()
        for c in range(2):
            rearrange(
                lambda g, j: last_in[f, c, strided(0, g, j), :],
                lambda g, j, x: out_store(handed_ref, other * nfh + f, c, g, j, x),
            )

    total = sum_own[...]
    for d in range(1, lateral):
        mate = device(section * lateral + lax.rem(place + d, lateral))
        remote(sum_own, sum_in.at[d], sum_sems, (d,), mate).wait_recv()
        total = total + sum_in[d]
    cells = length * lateral * blocks * LANES
    for l in range(LEVELS):
        mean = jnp.sum(total[l * SUB : (l + 1) * SUB], axis=(0, 1), keepdims=True) / cells
        scale = jnp.broadcast_to(1.0 / jnp.sqrt(mean + 1e-06), (SUB, LANES))

        def put(g, j, x):
            image_ref[l, pl.ds(g * SUB, SUB), pl.ds(j * LANES, LANES)] = x * scale

        rearrange(lambda g, j: raw_in[l, strided(0, g, j), :], put)

    for copy in swaps:
        copy.wait_send()
    for f in range(nfh):
        send_done = lambda make, stage: make(stage, f).wait_send()
        for stage in range(2 * LEVELS):
            live_up = has_up if stage < LEVELS else has_up & has_before
            live_down = has_down if stage < LEVELS else has_down & has_before
            pl.when(live_up)(lambda: send_done(halo_up, stage))
            pl.when(live_down)(lambda: send_done(halo_down, stage))

        @pl.when(has_after)
        def _():
            for copy in hand_parts(f):
                copy.wait_send()

        finish_wave(f).wait_send()
    for l in range(LEVELS):
        finish_raw(l).wait_send()
    for d in range(1, lateral):
        mate = device(section * lateral + lax.rem(place + d, lateral))
        remote(sum_own, sum_in.at[d], sum_sems, (d,), mate).wait_send()


def pltpu_store(ref, where, x):
    ref[where, :] = x


def out_store(ref, f, c, g, j, x):
    ref[f, c, pl.ds(g * SUB, SUB), pl.ds(j * LANES, LANES)] = x


def paired(
    incoming_wave,
    speed_class_map,
    spectral_entry_index,
    filter_weights,
    scaled_pulsations,
    inverse_speed_classes,
):
    strip_count = lax.axis_size("strip")
    lateral = strip_count // SECTIONS
    length = incoming_wave.shape[2]
    nfh = NFREQ // 2
    rows = 2 * length
    tall = (rows + 2 * ORDER + 2 * PAD) * SUB
    angle = scaled_pulsations[:, None] * inverse_speed_classes[None, :]
    cosine = jnp.cos(angle)[:, None, :]
    sine = jnp.sin(angle)[:, None, :]
    by_order = jnp.transpose(filter_weights, (2, 0, 3, 1))
    real = by_order[0] * cosine - by_order[1] * sine
    imag = by_order[0] * sine + by_order[1] * cosine
    table = jnp.stack([real, imag], axis=2).reshape(NW, 2 * (ORDER + 1), NBIN)
    table = jnp.pad(table, ((0, 0), (0, 0), (0, LANES - NBIN)))
    f32 = jnp.float32
    vmem = pl.BlockSpec(memory_space=pltpu.VMEM)

    def dma(*shape):
        return pltpu.SemaphoreType.DMA((2,) + shape)

    return pl.pallas_call(
        functools.partial(kernel, strip_count),
        out_shape=(
            jax.ShapeDtypeStruct(speed_class_map.shape, f32),
            jax.ShapeDtypeStruct(incoming_wave.shape, f32),
        ),
        in_specs=[pl.BlockSpec(memory_space=pltpu.SMEM), vmem, vmem, vmem],
        out_specs=(vmem, vmem),
        scratch_shapes=[
            pltpu.VMEM((2 * LEVELS, nfh, 2, tall, LANES), f32),
            pltpu.VMEM((ORDER, 2, tall, LANES), f32),
            pltpu.VMEM((nfh, 2, rows * SUB, LANES), f32),
            pltpu.VMEM((nfh, 2, rows * SUB, LANES), f32),
            pltpu.VMEM((nfh, 2, length * SUB, LANES), f32),
            pltpu.VMEM((nfh, 2, length * SUB, LANES), f32),
            pltpu.VMEM((LEVELS, length * SUB, LANES), jnp.int32),
            pltpu.VMEM((LEVELS, rows * SUB, LANES), jnp.int32),
            pltpu.VMEM((LEVELS, rows * SUB, LANES), f32),
            pltpu.VMEM((LEVELS, length * SUB, LANES), f32),
            pltpu.VMEM((LEVELS * SUB, LANES), f32),
            pltpu.VMEM((lateral, LEVELS * SUB, LANES), f32),
            dma(nfh + 1),
            dma(2 * LEVELS, nfh, 2),
            dma(nfh, 3),
            dma(nfh),
            dma(LEVELS),
            dma(lateral),
        ],
        compiler_params=pltpu.CompilerParams(
            collective_id=0, has_side_effects=True, vmem_limit_bytes=48 * 1024 * 1024
        ),
    )(spectral_entry_index, incoming_wave, speed_class_map, table)


def fits(mesh):
    lateral = mesh.shape["strip"] // SECTIONS
    return NFREQ % 2 == 0 and lateral % 4 == 0


def body_for(mesh):
    def body(wave, *rest):
        whole = wave.shape[3] == SUB * LANES and wave.shape[2] % SUB == 0
        if fits(mesh) and whole and wave.shape[2] >= ORDER:
            return paired(wave, *rest)
        return shards(wave, *rest)

    return body


def solution(mesh):
    return jax.shard_map(
        body_for(mesh),
        mesh=mesh,
        in_specs=(
            P("groups", None, "strip", None),
            P("groups", "strip", None),
            P("groups", None),
            P(),
            P(),
            P(),
        ),
        out_specs=(P("groups", "strip", None), P("groups", None, "strip", None)),
        check_vma=False,
    )
```

profile of v0, /device:TPU:1, one launch (start us, length us, event | category | flops | bytes accessed | tf_op | source)
XLA Modules:
  0.0 101.7 jit_solution(17472569692255793161)
XLA Ops:
  0.6 0.0 copy-start.3
  0.6 0.0 copy-start.4
  0.6 0.6 copy-done.3
  1.3 0.0 copy-done.4
  1.3 0.1 multiply_cosine_fusion
  1.4 1.3 %multiply_subtract_fusion = (f32[16,13,1,16]{3,2,1,0:T(1,128)S(1)}, f32[16,13,1,16]{3,2,1,0:T(1,128)S(1)}) fusion(f32[2,16,13,16]{3,0,2,1:T(2,128)} %bitcast.15, f32[16,16]{1,0:T(8,128)S(1)} %get-tuple-element.5, f32[16,16]{1,0:T(8,128)S(1)} %get-tuple-element.4), kind=kLoop, calls=%fused_computation.4 | loop fusion | flops 19968 | bytes 55296 | tf_op jit(solution)/shard_map/sub | solution.py:613
  2.7 0.2 pad_maximum_fusion
  3.0 0.0 copy-start
  3.0 0.1 copy.9
  3.1 0.0 copy-start.1
  3.1 0.0 copy-start.2
  3.1 0.9 copy-done
  4.0 0.0 copy-done.1
  4.1 0.0 copy-done.2
  4.1 96.2 %shard_map.77 = (f32[2,16,1024]{2,1,0:T(8,128)S(1)}, f32[4,2,16,1024]{3,2,1,0:T(8,128)S(1)}) custom-call(s32[4,4]{1,0:T(4,128)S(1)} %copy-done.2, f32[4,2,16,1024]{3,2,1,0:T(8,128)S(1)} %copy-done, s32[2,16,1024]{2,1,0:T(8,128)S(1)} %copy-done.1, f32[16,26,128]{2,1,0:T(8,128)S(1)} %pad.4.table_ref), custom_call_target="tpu_custom_call" | custom-call | tf_op jit(solution)/shard_map/pallas_call | solution.py:623
  100.3 0.7 copy.12
  100.9 0.8 copy.13
  (2 shorter events, 0.0 us)
Async XLA Ops:
  0.6 0.7 copy-start.3
  0.6 0.7 copy-start.4
  3.0 1.0 %copy-start = (f32[4,2,16,1024]{3,2,1,0:T(8,128)S(1)}, f32[4,2,16,1024]{3,2,1,0:T(8,128)}, u32[]{:S(2)}) copy-start(f32[4,2,16,1024]{3,2,1,0:T(8,128)} %wave_ref.1) | copy-start | bytes 1572868
  3.1 1.0 copy-start.1
  3.1 1.0 copy-start.2
where the time goes:
time: 102 us
  Pallas kernels  96.2 us (94%)
  local copies, waits for them, and re-layouts  3.17 us (3%)
  other arithmetic  1.64 us (2%)
    pallas_call x1, Pallas kernels, paired(): pl.pallas_call(functools.partial(kernel, strip_count), out_shape=(jax.Sha...  96.2 us
    unnamed x12, local copies, waits for them, and re-layouts  3.06 us

commit v1 on v0

--- a/solution.py
+++ b/solution.py
@@ -606,14 +606,7 @@
     nfh = NFREQ // 2
     rows = 2 * length
     tall = (rows + 2 * ORDER + 2 * PAD) * SUB
-    angle = scaled_pulsations[:, None] * inverse_speed_classes[None, :]
-    cosine = jnp.cos(angle)[:, None, :]
-    sine = jnp.sin(angle)[:, None, :]
-    by_order = jnp.transpose(filter_weights, (2, 0, 3, 1))
-    real = by_order[0] * cosine - by_order[1] * sine
-    imag = by_order[0] * sine + by_order[1] * cosine
-    table = jnp.stack([real, imag], axis=2).reshape(NW, 2 * (ORDER + 1), NBIN)
-    table = jnp.pad(table, ((0, 0), (0, 0), (0, LANES - NBIN)))
+    table = phase_table(filter_weights, scaled_pulsations, inverse_speed_classes)
     f32 = jnp.float32
     vmem = pl.BlockSpec(memory_space=pltpu.VMEM)
 
@@ -654,14 +647,469 @@
     )(spectral_entry_index, incoming_wave, speed_class_map, table)
 
 
+def transposed(x):
+    lane = lax.broadcasted_iota(jnp.int32, (SUB, LANES), 1)
+    x = list(x)
+    for step in (1, 2, 4):
+        odd = (lane // step) % 2 == 1
+        for a in range(8):
+            if (a // step) % 2 == 0:
+                low, high = x[a], x[a + step]
+                x[a] = jnp.where(odd, pltpu.roll(high, step, 1), low)
+                x[a + step] = jnp.where(odd, high, pltpu.roll(low, LANES - step, 1))
+    return x
+
+
+def quad_kernel(
+    strip_count,
+    entry_ref,
+    wave_ref,
+    map_ref,
+    table_ref,
+    image_ref,
+    handed_ref,
+    starts,
+    terms,
+    paired_sum,
+    running,
+    bottom,
+    wave_in,
+    map_in,
+    bins,
+    raw,
+    wave_out,
+    raw_out,
+    raw_in,
+    sum_own,
+    sum_in,
+    wave_sems,
+    map_sems,
+    relay_sems,
+    hand_sems,
+    fin_sems,
+    raw_sems,
+    sum_sems,
+    own_sems,
+):
+    length = wave_ref.shape[2]
+    groups = length // SUB
+    lateral = strip_count // SECTIONS
+    shift = lateral // 2
+    me = lax.axis_index("strip")
+    position = lax.rem(me + strip_count - shift, strip_count)
+    section = position // lateral
+    place = lax.rem(position, lateral)
+    chip = place // 2
+    core = lax.rem(place, 2)
+    has_before = section > 0
+    has_after = section < SECTIONS - 1
+    mates = {1: 2 * chip + 1 - core, 2: 2 * (1 - chip) + core, 3: 2 * (1 - chip) + 1 - core}
+
+    def device(pos):
+        return {"strip": lax.rem(pos + shift + strip_count, strip_count)}
+
+    def mate_device(mate):
+        return device(section * lateral + mate)
+
+    deeper = device(position + lateral)
+    shallower = device(position + strip_count - lateral)
+
+    def remote(src, dst, sems, index, target, arrival=None):
+        return pltpu.make_async_remote_copy(
+            src_ref=src,
+            dst_ref=dst,
+            send_sem=sems.at[(0,) + index],
+            recv_sem=sems.at[(1,) + (index if arrival is None else arrival)],
+            device_id=target,
+            device_id_type=MESH,
+        )
+
+    barrier = pltpu.get_barrier_semaphore()
+    for x in (1, 2, 3):
+        pl.semaphore_signal(
+            barrier, inc=1, device_id=mate_device(mates[x]), device_id_type=MESH
+        )
+    for target in (deeper, shallower):
+        pl.semaphore_signal(barrier, inc=1, device_id=target, device_id_type=MESH)
+    own_wave = pltpu.make_async_copy(wave_ref.at[place], wave_in.at[place], own_sems.at[0])
+    own_map = pltpu.make_async_copy(map_ref, map_in.at[place], own_sems.at[1])
+    own_wave.start()
+    own_map.start()
+    pl.semaphore_wait(barrier, lateral + 1)
+
+    def wave_copy(x):
+        return remote(
+            wave_ref.at[mates[x]], wave_in.at[place], wave_sems, (x,), mate_device(mates[x])
+        )
+
+    def map_copy(level, x):
+        return remote(
+            map_ref.at[level],
+            map_in.at[place, level],
+            map_sems,
+            (level, x),
+            mate_device(mates[x]),
+        )
+
+    def map_relay(level):
+        part = map_in.at[mates[2], level]
+        return remote(part, part, relay_sems, (level,), mate_device(mates[1]))
+
+    map_copy(0, 2).start()
+    wave_copy(2).start()
+    wave_copy(3).start()
+    map_copy(1, 2).start()
+    map_copy(0, 1).start()
+    wave_copy(1).start()
+    map_copy(1, 1).start()
+
+    lane = lax.broadcasted_iota(jnp.int32, (SUB, LANES), 1)
+    sub = lax.broadcasted_iota(jnp.int32, (SUB, LANES), 0)
+    low_lane, high_lane = lane // 8, lane % 8
+    to_left = jnp.where(low_lane > 0, lane - 8, jnp.where(high_lane > 0, 119 + high_lane, 0))
+    to_right = jnp.where(low_lane < 15, lane + 8, jnp.where(high_lane < 7, high_lane + 1, 127))
+    not_first_lane = lane > 0
+    not_last_lane = lane < LANES - 1
+    not_first_sub = sub > 0
+    not_last_sub = sub < SUB - 1
+
+    def cell(m, r):
+        return pl.ds((m * SUB + r) * SUB, SUB)
+
+    def lane_pick(x, index):
+        return jnp.take_along_axis(x, index, axis=1, mode="promise_in_bounds")
+
+    def spread(load, store):
+        out = transposed([load(j) for j in range(8)])
+        for m in range(8):
+            store(m, out[m])
+
+    def column(m, slot):
+        return pl.ds(m * SUB * SUB + slot, SUB, stride=SUB)
+
+    def spread_map(level):
+        for d in range(lateral):
+            for g in range(groups):
+                spread(
+                    lambda j: map_in[d, level, pl.ds(g * SUB, SUB), pl.ds(j * LANES, LANES)],
+                    lambda m, x: ref_store(bins.at[level], column(m, groups * d + g), x),
+                )
+
+    def spread_wave():
+        for d in range(lateral):
+            for c in range(2):
+                for g in range(groups):
+                    spread(
+                        lambda j: wave_in[d, c, pl.ds(g * SUB, SUB), pl.ds(j * LANES, LANES)],
+                        lambda m, x: ref_store(
+                            starts.at[0, c], column(m, groups * d + g), x
+                        ),
+                    )
+
+    def gather_back(source, d, g):
+        return transposed([source[column(m, groups * d + g), :] for m in range(8)])
+
+    def coefficient(entry, k, c):
+        return jnp.broadcast_to(table_ref[entry, pl.ds(2 * k + c, 1), :], (SUB, LANES))
+
+    def stencil_step(level, entry, k, present, target, first):
+        cr, ci = (coefficient(entry, k, c) for c in range(2))
+        below = [[None] * 8, [None] * 8]
+        for c in range(2):
+            for m in range(8):
+                edge = pltpu.roll(present[c, cell(m, 7), :], 1, 0)
+                edge = jnp.where(not_first_sub, edge, 0.0)
+                below[c][m] = edge + present[c, cell(m, 0), :]
+        for r in range(8):
+            for c in range(2):
+                u = []
+                for m in range(8):
+                    here = present[c, cell(m, r), :]
+                    if r < 7:
+                        above = present[c, cell(m, r + 1), :]
+                    else:
+                        above = pltpu.roll(present[c, cell(m, 0), :], SUB - 1, 0)
+                        above = jnp.where(not_last_sub, above, 0.0)
+                    q = here + above
+                    u.append(below[c][m] + q)
+                    below[c][m] = q
+                left = jnp.where(not_first_lane, lane_pick(u[7], to_left), 0.0)
+                right = jnp.where(not_last_lane, lane_pick(u[0], to_right), 0.0)
+                u = [left] + u + [right]
+                h = [u[m] + u[m + 1] for m in range(9)]
+                for m in range(8):
+                    w = h[m] + h[m + 1]
+                    here = present[c, cell(m, r), :]
+                    if first:
+                        both = 0.125 * w
+                    else:
+                        both = 0.25 * w - paired_sum[c, cell(m, r), :]
+                    paired_sum[c, cell(m, r), :] = both
+                    target[c, cell(m, r), :] = both - here
+            for m in range(8):
+                index = bins[level, cell(m, r), :]
+                br, bi = lane_pick(cr, index), lane_pick(ci, index)
+                tr, ti = (present[c, cell(m, r), :] for c in range(2))
+                re = br * tr - bi * ti
+                im = br * ti + bi * tr
+                if not first:
+                    re = running[0, cell(m, r), :] + re
+                    im = running[1, cell(m, r), :] + im
+                running[0, cell(m, r), :] = re
+                running[1, cell(m, r), :] = im
+
+    def unit(tick, level, output):
+        stage = tick * LEVELS + level
+        batch = section if tick == 0 else jnp.maximum(section - 1, 0)
+        entry = entry_ref[batch, place]
+        stencil_step(level, entry, 0, starts.at[stage], terms.at[1], True)
+
+        def step(k, carry):
+            stencil_step(
+                level, entry, k, terms.at[lax.rem(k, 2)], terms.at[lax.rem(k + 1, 2)], False
+            )
+            return carry
+
+        lax.fori_loop(1, ORDER, step, 0)
+        final = terms.at[ORDER % 2]
+        cr, ci = (coefficient(entry, ORDER, c) for c in range(2))
+        for r in range(8):
+            for m in range(8):
+                index = bins[level, cell(m, r), :]
+                br, bi = lane_pick(cr, index), lane_pick(ci, index)
+                tr, ti = (final[c, cell(m, r), :] for c in range(2))
+                re = running[0, cell(m, r), :] + (br * tr - bi * ti)
+                im = running[1, cell(m, r), :] + (br * ti + bi * tr)
+                output[0, cell(m, r), :] = re
+                output[1, cell(m, r), :] = im
+                if tick == 0:
+                    raw[level, cell(m, r), :] = re
+                else:
+                    raw[level, cell(m, r), :] = raw[level, cell(m, r), :] + re
+
+    def hand():
+        return remote(bottom, starts.at[LEVELS], hand_sems, (), deeper)
+
+    def finish_raw(level, d):
+        return remote(
+            raw_out.at[level, d],
+            raw_in.at[level, place],
+            raw_sems,
+            (level, d),
+            mate_device(d),
+            (level, place),
+        )
+
+    def raw_arrival(level, f):
+        return remote(
+            raw_out.at[level, f], raw_in.at[level, f], raw_sems, (level, f), mate_device(f)
+        )
+
+    def finish_wave(d):
+        return remote(
+            wave_out.at[d], handed_ref.at[place], fin_sems, (d,), mate_device(d), (place,)
+        )
+
+    def wave_arrival(f):
+        return remote(wave_out.at[f], handed_ref.at[f], fin_sems, (f,), mate_device(f))
+
+    def send_raw(level):
+        for d in range(lateral):
+            for g in range(groups):
+                for j, x in enumerate(gather_back(raw.at[level], d, g)):
+                    raw_out[level, d, pl.ds(g * SUB, SUB), pl.ds(j * LANES, LANES)] = x
+            pl.when(place != d)(lambda: finish_raw(level, d).start())
+
+    own_map.wait()
+    map_copy(0, 2).wait_recv()
+    map_relay(0).start()
+    map_copy(0, 1).wait_recv()
+    map_relay(0).wait_recv()
+    spread_map(0)
+    own_wave.wait()
+    for x in (1, 2, 3):
+        wave_copy(x).wait_recv()
+    spread_wave()
+    unit(0, 0, starts.at[1])
+    map_copy(1, 2).wait_recv()
+    map_relay(1).start()
+    map_copy(1, 1).wait_recv()
+    map_relay(1).wait_recv()
+    spread_map(1)
+    unit(0, 1, bottom)
+    pl.when(has_after)(lambda: hand().start())
+
+    @pl.when(has_before)
+    def _():
+        hand().wait_recv()
+        unit(1, 0, starts.at[LEVELS + 1])
+
+    send_raw(0)
+    pl.when(has_after)(lambda: hand().wait_send())
+
+    @pl.when(has_before)
+    def _():
+        unit(1, 1, bottom)
+
+    send_raw(1)
+    for d in range(lateral):
+        for c in range(2):
+            for g in range(groups):
+                for j, x in enumerate(gather_back(bottom.at[c], d, g)):
+                    wave_out[d, c, pl.ds(g * SUB, SUB), pl.ds(j * LANES, LANES)] = x
+        pl.when(place != d)(lambda: finish_wave(d).start())
+    own_out = pltpu.make_async_copy(wave_out.at[place], handed_ref.at[place], own_sems.at[0])
+    own_out.start()
+    for level in range(LEVELS):
+        own_raw = pltpu.make_async_copy(
+            raw_out.at[level, place], raw_in.at[level, place], own_sems.at[1]
+        )
+        own_raw.start()
+        own_raw.wait()
+        for f in range(lateral):
+            pl.when(place != f)(lambda: raw_arrival(level, f).wait_recv())
+
+        def merge(g, total):
+            row = pl.ds(pl.multiple_of(g * SUB, SUB), SUB)
+            for j in range(8):
+                col = pl.ds(j * LANES, LANES)
+                value = raw_in[level, 0, row, col]
+                for f in range(1, lateral):
+                    value = value + raw_in[level, f, row, col]
+                raw_in[level, 0, row, col] = value
+                total = total + value * value
+            return total
+
+        sum_own[pl.ds(level * SUB, SUB), :] = lax.fori_loop(
+            0, groups, merge, jnp.zeros((SUB, LANES), jnp.float32)
+        )
+    for x in (1, 2, 3):
+        remote(sum_own, sum_in.at[x], sum_sems, (x,), mate_device(mates[x])).start()
+    total = sum_own[...]
+    for x in (1, 2, 3):
+        remote(sum_own, sum_in.at[x], sum_sems, (x,), mate_device(mates[x])).wait_recv()
+        total = total + sum_in[x]
+    cells = length * lateral * SUB * LANES
+    for level in range(LEVELS):
+        mean = (
+            jnp.sum(total[level * SUB : (level + 1) * SUB], axis=(0, 1), keepdims=True) / cells
+        )
+        scale = jnp.broadcast_to(1.0 / jnp.sqrt(mean + 1e-06), (SUB, LANES))
+        for g in range(groups):
+            for j in range(8):
+                row, col = pl.ds(g * SUB, SUB), pl.ds(j * LANES, LANES)
+                image_ref[level, row, col] = raw_in[level, 0, row, col] * scale
+    own_out.wait()
+    for f in range(lateral):
+        pl.when(place != f)(lambda: wave_arrival(f).wait_recv())
+    for x in (1, 2, 3):
+        wave_copy(x).wait_send()
+        remote(sum_own, sum_in.at[x], sum_sems, (x,), mate_device(mates[x])).wait_send()
+    for level in range(LEVELS):
+        for x in (1, 2):
+            map_copy(level, x).wait_send()
+        map_relay(level).wait_send()
+    for d in range(lateral):
+
+        @pl.when(place != d)
+        def _():
+            finish_wave(d).wait_send()
+            for level in range(LEVELS):
+                finish_raw(level, d).wait_send()
+
+
+def ref_store(ref, where, x):
+    ref[where, :] = x
+
+
+def phase_table(filter_weights, scaled_pulsations, inverse_speed_classes):
+    angle = scaled_pulsations[:, None] * inverse_speed_classes[None, :]
+    cosine = jnp.cos(angle)[:, None, :]
+    sine = jnp.sin(angle)[:, None, :]
+    by_order = jnp.transpose(filter_weights, (2, 0, 3, 1))
+    real = by_order[0] * cosine - by_order[1] * sine
+    imag = by_order[0] * sine + by_order[1] * cosine
+    table = jnp.stack([real, imag], axis=2).reshape(NW, 2 * (ORDER + 1), NBIN)
+    return jnp.pad(table, ((0, 0), (0, 0), (0, LANES - NBIN)))
+
+
+def quads(
+    incoming_wave,
+    speed_class_map,
+    spectral_entry_index,
+    filter_weights,
+    scaled_pulsations,
+    inverse_speed_classes,
+):
+    strip_count = lax.axis_size("strip")
+    lateral = strip_count // SECTIONS
+    length, across = incoming_wave.shape[2:]
+    tall = length * lateral * SUB
+    f32 = jnp.float32
+    vmem = pl.BlockSpec(memory_space=pltpu.VMEM)
+
+    def dma(*shape):
+        return pltpu.SemaphoreType.DMA((2,) + shape)
+
+    return pl.pallas_call(
+        functools.partial(quad_kernel, strip_count),
+        out_shape=(
+            jax.ShapeDtypeStruct(speed_class_map.shape, f32),
+            jax.ShapeDtypeStruct(incoming_wave.shape, f32),
+        ),
+        in_specs=[pl.BlockSpec(memory_space=pltpu.SMEM), vmem, vmem, vmem],
+        out_specs=(vmem, vmem),
+        scratch_shapes=[
+            pltpu.VMEM((2 * LEVELS, 2, tall, LANES), f32),
+            pltpu.VMEM((2, 2, tall, LANES), f32),
+            pltpu.VMEM((2, tall, LANES), f32),
+            pltpu.VMEM((2, tall, LANES), f32),
+            pltpu.VMEM((2, tall, LANES), f32),
+            pltpu.VMEM((lateral, 2, length, across), f32),
+            pltpu.VMEM((lateral, LEVELS, length, across), jnp.int32),
+            pltpu.VMEM((LEVELS, tall, LANES), jnp.int32),
+            pltpu.VMEM((LEVELS, tall, LANES), f32),
+            pltpu.VMEM((lateral, 2, length, across), f32),
+            pltpu.VMEM((LEVELS, lateral, length, across), f32),
+            pltpu.VMEM((LEVELS, lateral, length, across), f32),
+            pltpu.VMEM((LEVELS * SUB, LANES), f32),
+            pltpu.VMEM((lateral, LEVELS * SUB, LANES), f32),
+            dma(lateral),
+            dma(LEVELS, lateral),
+            dma(LEVELS),
+            dma(),
+            dma(lateral),
+            dma(LEVELS, lateral),
+            dma(lateral),
+            pltpu.SemaphoreType.DMA((2,)),
+        ],
+        compiler_params=pltpu.CompilerParams(
+            collective_id=0, has_side_effects=True, vmem_limit_bytes=48 * 1024 * 1024
+        ),
+    )(
+        spectral_entry_index,
+        incoming_wave,
+        speed_class_map,
+        phase_table(filter_weights, scaled_pulsations, inverse_speed_classes),
+    )
+
+
 def fits(mesh):
     lateral = mesh.shape["strip"] // SECTIONS
     return NFREQ % 2 == 0 and lateral % 4 == 0
 
 
+def whole_section(mesh, wave):
+    lateral = mesh.shape["strip"] // SECTIONS
+    full = lateral * wave.shape[2] == SUB * SUB and wave.shape[3] == SUB * LANES
+    return lateral == NFREQ == 4 and wave.shape[2] % SUB == 0 and full
+
+
 def body_for(mesh):
     def body(wave, *rest):
         whole = wave.shape[3] == SUB * LANES and wave.shape[2] % SUB == 0
+        if whole_section(mesh, wave):
+            return quads(wave, *rest)
         if fits(mesh) and whole and wave.shape[2] >= ORDER:
             return paired(wave, *rest)
         return shards(wave, *rest)

time: 102 us -> 78.7 us (0.77)
  Pallas kernels: 96.2 us -> 72.6 us
    pallas_call x1, Pallas kernels: 96.2 us -> 72.6 us  [quads(): pl.pallas_call(functools.partial(quad_kernel, strip_count), out_shape=(ja...]
where the time goes in v1:
time: 78.7 us; the launch traced here: 78.1 us
  Pallas kernels  72.6 us (92%)
  local copies, waits for them, and re-layouts  3.17 us (4%)
  other arithmetic  1.64 us (2%)
    pallas_call x1, Pallas kernels, quads(): pl.pallas_call(functools.partial(quad_kernel, strip_count), out_shape=(ja...  72.6 us
    unnamed x12, local copies, waits for them, and re-layouts  3.06 us

profile of v1, /device:TPU:1, one launch (start us, length us, event | category | flops | bytes accessed | tf_op | source)
XLA Modules:
  0.0 78.1 jit_solution(3992226402865034031)
XLA Ops:
  0.6 0.0 copy-start.3
  0.6 0.0 copy-start.4
  0.6 0.6 copy-done.3
  1.3 0.0 copy-done.4
  1.3 0.1 multiply_cosine_fusion
  1.4 1.3 %multiply_subtract_fusion = (f32[16,13,1,16]{3,2,1,0:T(1,128)S(1)}, f32[16,13,1,16]{3,2,1,0:T(1,128)S(1)}) fusion(f32[2,16,13,16]{3,0,2,1:T(2,128)} %bitcast.15, f32[16,16]{1,0:T(8,128)S(1)} %get-tuple-element.5, f32[16,16]{1,0:T(8,128)S(1)} %get-tuple-element.4), kind=kLoop, calls=%fused_computation.4 | loop fusion | flops 19968 | bytes 55296 | tf_op jit(solution)/shard_map/sub | solution.py:1030
  2.7 0.2 pad_maximum_fusion
  3.0 0.0 copy-start
  3.0 0.1 copy.9
  3.1 0.0 copy-start.1
  3.1 0.0 copy-start.2
  3.1 0.9 %copy-done = f32[4,2,16,1024]{3,2,1,0:T(8,128)S(1)} copy-done((f32[4,2,16,1024]{3,2,1,0:T(8,128)S(1)}, f32[4,2,16,1024]{3,2,1,0:T(8,128)}, u32[]{:S(2)}) %copy-start) | copy-done | bytes 524312
  4.0 0.0 copy-done.1
  4.1 0.0 copy-done.2
  4.1 72.6 %shard_map.77 = (f32[2,16,1024]{2,1,0:T(8,128)S(1)}, f32[4,2,16,1024]{3,2,1,0:T(8,128)S(1)}) custom-call(s32[4,4]{1,0:T(4,128)S(1)} %copy-done.2, f32[4,2,16,1024]{3,2,1,0:T(8,128)S(1)} %copy-done, s32[2,16,1024]{2,1,0:T(8,128)S(1)} %copy-done.1, f32[16,26,128]{2,1,0:T(8,128)S(1)} %pad.4.table_ref), custom_call_target="tpu_custom_call" | custom-call | tf_op jit(solution)/shard_map/pallas_call | solution.py:1054
  76.7 0.7 copy.12
  77.4 0.8 %copy.13 = f32[4,2,16,1024]{3,2,1,0:T(8,128)} copy(f32[4,2,16,1024]{3,2,1,0:T(8,128)S(1)} %get-tuple-element.9) | data formatting | bytes 1048576
  (2 shorter events, 0.0 us)
Async XLA Ops:
  0.6 0.7 copy-start.3
  0.6 0.7 copy-start.4
  3.0 1.0 %copy-start = (f32[4,2,16,1024]{3,2,1,0:T(8,128)S(1)}, f32[4,2,16,1024]{3,2,1,0:T(8,128)}, u32[]{:S(2)}) copy-start(f32[4,2,16,1024]{3,2,1,0:T(8,128)} %wave_ref.1) | copy-start | bytes 1572868
  3.1 1.0 %copy-start.1 = (s32[2,16,1024]{2,1,0:T(8,128)S(1)}, s32[2,16,1024]{2,1,0:T(8,128)}, u32[]{:S(2)}) copy-start(s32[2,16,1024]{2,1,0:T(8,128)} %map_ref.1) | copy-start | bytes 393220
  3.1 1.0 %copy-start.2 = (s32[4,4]{1,0:T(4,128)S(1)}, s32[4,4]{1,0:T(4,128)}, u32[]{:S(2)}) copy-start(s32[4,4]{1,0:T(4,128)} %entry_ref.1) | copy-start | bytes 196

commit v2 on v1

--- a/solution.py
+++ b/solution.py
@@ -647,6 +647,9 @@
     )(spectral_entry_index, incoming_wave, speed_class_map, table)
 
 
+ROWS = 2 * (ORDER + 1)
+
+
 def transposed(x):
     lane = lax.broadcasted_iota(jnp.int32, (SUB, LANES), 1)
     x = list(x)
@@ -669,9 +672,12 @@
     image_ref,
     handed_ref,
     starts,
-    terms,
+    even,
+    odd,
     paired_sum,
     running,
+    coeffs,
+    spread_table,
     bottom,
     wave_in,
     map_in,
@@ -777,7 +783,9 @@
         return pl.ds((m * SUB + r) * SUB, SUB)
 
     def lane_pick(x, index):
-        return jnp.take_along_axis(x, index, axis=1, mode="promise_in_bounds")
+        return jnp.take_along_axis(
+            x, index, axis=1, mode="promise_in_bounds", wrap_negative_indices=False
+        )
 
     def spread(load, store):
         out = transposed([load(j) for j in range(8)])
@@ -809,19 +817,43 @@
     def gather_back(source, d, g):
         return transposed([source[column(m, groups * d + g), :] for m in range(8)])
 
-    def coefficient(entry, k, c):
-        return jnp.broadcast_to(table_ref[entry, pl.ds(2 * k + c, 1), :], (SUB, LANES))
-
-    def stencil_step(level, entry, k, present, target, first):
-        cr, ci = (coefficient(entry, k, c) for c in range(2))
-        below = [[None] * 8, [None] * 8]
-        for c in range(2):
+    def fill(level, tick):
+        batch = section if tick == 0 else jnp.maximum(section - 1, 0)
+        entry = entry_ref[batch, place]
+        for half in range(2):
+            block = table_ref[entry, pl.ds(half * SUB, SUB), :]
+            for n in range(ROWS):
+                spread_table[half, n] = jnp.broadcast_to(block[:, n : n + 1], (SUB, LANES))
+
+        def one(i, carry):
+            where = pl.ds(pl.multiple_of(i * SUB, SUB), SUB)
+            bin_ = bins[level, where, :]
+            high = bin_ >= SUB
+            low_bits = bin_ % SUB
+            for n in range(ROWS):
+                a, b = (
+                    jnp.take_along_axis(
+                        spread_table[half, n],
+                        low_bits,
+                        axis=0,
+                        mode="promise_in_bounds",
+                        wrap_negative_indices=False,
+                    )
+                    for half in range(2)
+                )
+                coeffs[level, n, where, :] = jnp.where(high, b, a)
+            return carry
+
+        lax.fori_loop(0, SUB * SUB, one, 0)
+
+    def stencil(present, target, first=False, last=False):
+        def channel(c, carry):
+            below = []
             for m in range(8):
                 edge = pltpu.roll(present[c, cell(m, 7), :], 1, 0)
                 edge = jnp.where(not_first_sub, edge, 0.0)
-                below[c][m] = edge + present[c, cell(m, 0), :]
-        for r in range(8):
-            for c in range(2):
+                below.append(edge + present[c, cell(m, 0), :])
+            for r in range(8):
                 u = []
                 for m in range(8):
                     here = present[c, cell(m, r), :]
@@ -831,8 +863,8 @@
                         above = pltpu.roll(present[c, cell(m, 0), :], SUB - 1, 0)
                         above = jnp.where(not_last_sub, above, 0.0)
                     q = here + above
-                    u.append(below[c][m] + q)
-                    below[c][m] = q
+                    u.append(below[m] + q)
+                    below[m] = q
                 left = jnp.where(not_first_lane, lane_pick(u[7], to_left), 0.0)
                 right = jnp.where(not_last_lane, lane_pick(u[0], to_right), 0.0)
                 u = [left] + u + [right]
@@ -844,48 +876,59 @@
                         both = 0.125 * w
                     else:
                         both = 0.25 * w - paired_sum[c, cell(m, r), :]
-                    paired_sum[c, cell(m, r), :] = both
+                    if not last:
+                        paired_sum[c, cell(m, r), :] = both
                     target[c, cell(m, r), :] = both - here
-            for m in range(8):
-                index = bins[level, cell(m, r), :]
-                br, bi = lane_pick(cr, index), lane_pick(ci, index)
-                tr, ti = (present[c, cell(m, r), :] for c in range(2))
-                re = br * tr - bi * ti
-                im = br * ti + bi * tr
-                if not first:
-                    re = running[0, cell(m, r), :] + re
-                    im = running[1, cell(m, r), :] + im
-                running[0, cell(m, r), :] = re
-                running[1, cell(m, r), :] = im
+            return carry
+
+        lax.fori_loop(0, 2, channel, 0)
+
+    def add_orders(level, terms, where, total):
+        re, im = (None, None) if total is None else total
+        for order, ref in terms:
+            tr, ti = (ref[c, where, :] for c in range(2))
+            br = coeffs[level, order, where, :]
+            bi = coeffs[level, ORDER + 1 + order, where, :]
+            dr = br * tr - bi * ti
+            di = br * ti + bi * tr
+            re, im = (dr, di) if re is None else (re + dr, im + di)
+        return re, im
+
+    def sum_so_far(where):
+        return [running[c, where, :] for c in range(2)]
 
     def unit(tick, level, output):
-        stage = tick * LEVELS + level
-        batch = section if tick == 0 else jnp.maximum(section - 1, 0)
-        entry = entry_ref[batch, place]
-        stencil_step(level, entry, 0, starts.at[stage], terms.at[1], True)
-
-        def step(k, carry):
-            stencil_step(
-                level, entry, k, terms.at[lax.rem(k, 2)], terms.at[lax.rem(k + 1, 2)], False
-            )
+        start = starts.at[tick * LEVELS + level]
+        stencil(start, odd, first=True)
+        for i in range(SUB * SUB):
+            where = pl.ds(i * SUB, SUB)
+            total = add_orders(level, [(0, start), (1, odd)], where, None)
+            for c in range(2):
+                running[c, where, :] = total[c]
+
+        def steps(i, carry):
+            stencil(odd, even)
+            stencil(even, odd)
+            for n in range(SUB * SUB):
+                where = pl.ds(n * SUB, SUB)
+                terms = [(2 * i + 2, even), (2 * i + 3, odd)]
+                total = add_orders(level, terms, where, sum_so_far(where))
+                for c in range(2):
+                    running[c, where, :] = total[c]
             return carry
 
-        lax.fori_loop(1, ORDER, step, 0)
-        final = terms.at[ORDER % 2]
-        cr, ci = (coefficient(entry, ORDER, c) for c in range(2))
-        for r in range(8):
-            for m in range(8):
-                index = bins[level, cell(m, r), :]
-                br, bi = lane_pick(cr, index), lane_pick(ci, index)
-                tr, ti = (final[c, cell(m, r), :] for c in range(2))
-                re = running[0, cell(m, r), :] + (br * tr - bi * ti)
-                im = running[1, cell(m, r), :] + (br * ti + bi * tr)
-                output[0, cell(m, r), :] = re
-                output[1, cell(m, r), :] = im
+        lax.fori_loop(0, ORDER // 2 - 1, steps, 0)
+        stencil(odd, even, last=True)
+        for r in range(SUB):
+            for m in range(SUB):
+                where = cell(m, r)
+                total = add_orders(level, [(ORDER, even)], where, sum_so_far(where))
+                for c in range(2):
+                    output[c, where, :] = total[c]
                 if tick == 0:
-                    raw[level, cell(m, r), :] = re
+                    raw[level, where, :] = total[0]
                 else:
-                    raw[level, cell(m, r), :] = raw[level, cell(m, r), :] + re
+                    raw[level, where, :] = raw[level, where, :] + total[0]
 
     def hand():
         return remote(bottom, starts.at[LEVELS], hand_sems, (), deeper)
@@ -926,6 +969,7 @@
     map_copy(0, 1).wait_recv()
     map_relay(0).wait_recv()
     spread_map(0)
+    fill(0, 0)
     own_wave.wait()
     for x in (1, 2, 3):
         wave_copy(x).wait_recv()
@@ -936,11 +980,14 @@
     map_copy(1, 1).wait_recv()
     map_relay(1).wait_recv()
     spread_map(1)
+    fill(1, 0)
     unit(0, 1, bottom)
     pl.when(has_after)(lambda: hand().start())
 
     @pl.when(has_before)
     def _():
+        fill(0, 1)
+        fill(1, 1)
         hand().wait_recv()
         unit(1, 0, starts.at[LEVELS + 1])
 
@@ -1022,14 +1069,16 @@
     ref[where, :] = x
 
 
-def phase_table(filter_weights, scaled_pulsations, inverse_speed_classes):
-    angle = scaled_pulsations[:, None] * inverse_speed_classes[None, :]
-    cosine = jnp.cos(angle)[:, None, :]
-    sine = jnp.sin(angle)[:, None, :]
-    by_order = jnp.transpose(filter_weights, (2, 0, 3, 1))
-    real = by_order[0] * cosine - by_order[1] * sine
-    imag = by_order[0] * sine + by_order[1] * cosine
-    table = jnp.stack([real, imag], axis=2).reshape(NW, 2 * (ORDER + 1), NBIN)
+def turned(filter_weights, scaled_pulsations, inverse_speed_classes):
+    angle = scaled_pulsations[:, None, None] * inverse_speed_classes[None, :, None]
+    cosine, sine = jnp.cos(angle), jnp.sin(angle)
+    real, imag = filter_weights[:, :, 0], filter_weights[:, :, 1]
+    return real * cosine - imag * sine, real * sine + imag * cosine
+
+
+def phase_table(*tables):
+    table = jnp.transpose(jnp.stack(turned(*tables), axis=3), (0, 2, 3, 1))
+    table = table.reshape(NW, 2 * (ORDER + 1), NBIN)
     return jnp.pad(table, ((0, 0), (0, 0), (0, LANES - NBIN)))
 
 
@@ -1061,9 +1110,12 @@
         out_specs=(vmem, vmem),
         scratch_shapes=[
             pltpu.VMEM((2 * LEVELS, 2, tall, LANES), f32),
-            pltpu.VMEM((2, 2, tall, LANES), f32),
             pltpu.VMEM((2, tall, LANES), f32),
             pltpu.VMEM((2, tall, LANES), f32),
+            pltpu.VMEM((2, tall, LANES), f32),
+            pltpu.VMEM((2, tall, LANES), f32),
+            pltpu.VMEM((LEVELS, ROWS, tall, LANES), f32),
+            pltpu.VMEM((2, ROWS, SUB, LANES), f32),
             pltpu.VMEM((2, tall, LANES), f32),
             pltpu.VMEM((lateral, 2, length, across), f32),
             pltpu.VMEM((lateral, LEVELS, length, across), jnp.int32),
@@ -1090,7 +1142,9 @@
         spectral_entry_index,
         incoming_wave,
         speed_class_map,
-        phase_table(filter_weights, scaled_pulsations, inverse_speed_classes),
+        jnp.concatenate(
+            turned(filter_weights, scaled_pulsations, inverse_speed_classes), axis=2
+        ),
     )
 
 

time: 78.7 us -> 64.4 us (0.82)
  Pallas kernels: 72.6 us -> 58.3 us
    pallas_call x1, Pallas kernels: 72.6 us -> 58.3 us  [quads(): pl.pallas_call(functools.partial(quad_kernel, strip_count), out_shape=(ja...]
    slice x0 -> x1, local copies, waits for them, and re-layouts: none -> 1.22 us  [turned(): real, imag = (filter_weights[:, :, 0], filter_weights[:, :, 1])]
    sub x1, other arithmetic: 1.28 us -> 0.13 us  [turned(): return (real * cosine - imag * sine, real * sine + imag * cosine)]
    unnamed x12 -> x10, local copies, waits for them, and re-layouts: 3.06 us -> 2.62 us
where the time goes in v2:
time: 64.4 us; the launch traced here: 63.9 us
  Pallas kernels  58.3 us (91%)
  local copies, waits for them, and re-layouts  3.84 us (6%)
  other arithmetic  1.02 us (2%)
  between operations  0.68 us (1%)
    pallas_call x1, Pallas kernels, quads(): pl.pallas_call(functools.partial(quad_kernel, strip_count), out_shape=(ja...  58.3 us
    unnamed x10, local copies, waits for them, and re-layouts  2.62 us

profile of v2, /device:TPU:1, one launch (start us, length us, event | category | flops | bytes accessed | tf_op | source)
XLA Modules:
  0.0 63.9 jit_solution(9223813362011240554)
XLA Ops:
  0.6 0.8 %multiply_cosine_fusion = (f32[16,16]{1,0:T(8,128)S(1)}, f32[16,16]{1,0:T(8,128)S(1)}) fusion(f32[16]{0:T(128)} %param.11, f32[16]{0:T(128)} %param.10), kind=kLoop, calls=%fused_computation.8 | loop fusion | flops 256 | bytes 2176 | tf_op jit(solution)/shard_map/cos | solution.py:1074
  1.4 1.2 %fusion.2 = (f32[16,16,1,13]{1,2,3,0:T(1,128)S(1)}, f32[16,16,1,13]{1,2,3,0:T(1,128)S(1)}) fusion(f32[16,16,2,13]{1,2,3,0:T(2,128)} %param.9), kind=kLoop, calls=%fused_computation.9 | loop fusion | bytes 53248 | tf_op jit(solution)/shard_map/slice | solution.py:1075
  2.6 0.2 copy.10
  2.8 0.2 copy.11
  3.0 0.0 copy-start
  3.0 0.1 fusion
  3.1 0.0 copy-start.1
  3.1 0.0 copy-start.2
  3.2 0.1 pad_maximum_fusion.table_ref
  3.3 0.8 %copy-done = f32[4,2,16,1024]{3,2,1,0:T(8,128)S(1)} copy-done((f32[4,2,16,1024]{3,2,1,0:T(8,128)S(1)}, f32[4,2,16,1024]{3,2,1,0:T(8,128)}, u32[]{:S(2)}) %copy-start) | copy-done | bytes 524312
  4.0 0.1 copy-done.1
  4.1 0.0 copy-done.2
  4.1 58.3 %shard_map.77 = (f32[2,16,1024]{2,1,0:T(8,128)S(1)}, f32[4,2,16,1024]{3,2,1,0:T(8,128)S(1)}) custom-call(s32[4,4]{1,0:T(4,128)S(1)} %copy-done.2, f32[4,2,16,1024]{3,2,1,0:T(8,128)S(1)} %copy-done, s32[2,16,1024]{2,1,0:T(8,128)S(1)} %copy-done.1, f32[16,16,26]{2,1,0:T(8,128)S(1)} %pad_maximum_fusion.table_ref), custom_call_target="tpu_custom_call" | custom-call | tf_op jit(solution)/shard_map/pallas_call | solution.py:1103
  62.4 0.7 %copy.14 = f32[2,16,1024]{2,1,0:T(8,128)} copy(f32[2,16,1024]{2,1,0:T(8,128)S(1)} %get-tuple-element.10) | data formatting | bytes 262144
  63.1 0.8 %copy.15 = f32[4,2,16,1024]{3,2,1,0:T(8,128)} copy(f32[4,2,16,1024]{3,2,1,0:T(8,128)S(1)} %get-tuple-element.11) | data formatting | bytes 1048576
Async XLA Ops:
  3.0 1.0 %copy-start = (f32[4,2,16,1024]{3,2,1,0:T(8,128)S(1)}, f32[4,2,16,1024]{3,2,1,0:T(8,128)}, u32[]{:S(2)}) copy-start(f32[4,2,16,1024]{3,2,1,0:T(8,128)} %wave_ref.1) | copy-start | bytes 1572868
  3.1 1.0 %copy-start.1 = (s32[2,16,1024]{2,1,0:T(8,128)S(1)}, s32[2,16,1024]{2,1,0:T(8,128)}, u32[]{:S(2)}) copy-start(s32[2,16,1024]{2,1,0:T(8,128)} %map_ref.1) | copy-start | bytes 393220
  3.1 0.9 %copy-start.2 = (s32[4,4]{1,0:T(4,128)S(1)}, s32[4,4]{1,0:T(4,128)}, u32[]{:S(2)}) copy-start(s32[4,4]{1,0:T(4,128)} %entry_ref.1) | copy-start | bytes 196

commit v3 on v0

--- a/solution.py
+++ b/solution.py
@@ -606,14 +606,7 @@
     nfh = NFREQ // 2
     rows = 2 * length
     tall = (rows + 2 * ORDER + 2 * PAD) * SUB
-    angle = scaled_pulsations[:, None] * inverse_speed_classes[None, :]
-    cosine = jnp.cos(angle)[:, None, :]
-    sine = jnp.sin(angle)[:, None, :]
-    by_order = jnp.transpose(filter_weights, (2, 0, 3, 1))
-    real = by_order[0] * cosine - by_order[1] * sine
-    imag = by_order[0] * sine + by_order[1] * cosine
-    table = jnp.stack([real, imag], axis=2).reshape(NW, 2 * (ORDER + 1), NBIN)
-    table = jnp.pad(table, ((0, 0), (0, 0), (0, LANES - NBIN)))
+    table = phase_table(filter_weights, scaled_pulsations, inverse_speed_classes)
     f32 = jnp.float32
     vmem = pl.BlockSpec(memory_space=pltpu.VMEM)
 
@@ -654,14 +647,604 @@
     )(spectral_entry_index, incoming_wave, speed_class_map, table)
 
 
+ROWS = 2 * (ORDER + 1)
+TICKS = 2
+
+
+def lane_pick(x, index):
+    return jnp.take_along_axis(
+        x, index, axis=1, mode="promise_in_bounds", wrap_negative_indices=False
+    )
+
+
+def transposed(x):
+    lane = lax.broadcasted_iota(jnp.int32, (SUB, LANES), 1)
+    low = lane % SUB
+    bits = [(step, (lane // step) % 2 == 1) for step in (1, 2, 4)]
+    x = list(x)
+    for step, bit in bits:
+        x = [jnp.where(bit, x[(a + step) % SUB], x[a]) for a in range(SUB)]
+    for a in range(1, SUB):
+        x[a] = lane_pick(x[a], lane - low + (low + SUB - a) % SUB)
+    x = [x[-n % SUB] for n in range(SUB)]
+    for step, bit in bits:
+        x = [jnp.where(bit, x[(m - step) % SUB], x[m]) for m in range(SUB)]
+    return x
+
+
+def chain_kernel(
+    count,
+    entry_ref,
+    pulsation_ref,
+    slowness_ref,
+    weight_ref,
+    wave_ref,
+    map_ref,
+    image_ref,
+    handed_ref,
+    starts,
+    last,
+    even,
+    odd,
+    paired_sum,
+    running,
+    coeffs,
+    spread_table,
+    wave_in,
+    map_in,
+    bins,
+    raw,
+    wave_out,
+    raw_out,
+    raw_in,
+    sum_own,
+    sum_in,
+    wave_sems,
+    map_sems,
+    relay_sems,
+    fin_sems,
+    raw_sems,
+    sum_sems,
+    own_sems,
+    own_raw_sems,
+):
+    length = wave_ref.shape[2]
+    groups = length // SUB
+    lateral = count // SECTIONS
+    half = lateral // 2
+    me = lax.axis_index("strip")
+    plane = me // lateral
+    place = lax.rem(me, lateral)
+    side = place // 2
+    core = lax.rem(place, 2)
+    chain = lax.rem(plane + SECTIONS - 1, SECTIONS)
+    section = lax.rem(chain + side, SECTIONS)
+    slab = lax.rem(place + half, lateral)
+    home = lax.rem(section + 1, SECTIONS)
+    near = side == 0
+    has_next = chain < SECTIONS - 1
+    is_deep = section > 0
+
+    def wrapped(index):
+        return lax.rem(index + count, count)
+
+    def device(index):
+        return {"strip": wrapped(index)}
+
+    def worker(plane_, f):
+        return wrapped(plane_ * lateral + f)
+
+    def owner(section_, d):
+        return wrapped(section_ * lateral + half + d)
+
+    partner = device(me + 1 - 2 * core)
+
+    def remote(src, dst, sems, index, target, arrival=None):
+        return pltpu.make_async_remote_copy(
+            src_ref=src,
+            dst_ref=dst,
+            send_sem=sems.at[(0,) + index],
+            recv_sem=sems.at[(1,) + (index if arrival is None else arrival)],
+            device_id=target,
+            device_id_type=MESH,
+        )
+
+    barrier = pltpu.get_barrier_semaphore()
+    base = (plane - 1) * lateral
+    for n in range(3 * lateral):
+        mate = wrapped(base + n)
+
+        @pl.when(mate != me)
+        def _():
+            pl.semaphore_signal(barrier, inc=1, device_id=device(mate), device_id_type=MESH)
+
+    own_wave = pltpu.make_async_copy(wave_ref.at[place], wave_in.at[slab], own_sems.at[0])
+    own_map = pltpu.make_async_copy(map_ref, map_in.at[side, slab], own_sems.at[1])
+    pl.when(near)(own_wave.start)
+    pl.when(near | has_next)(own_map.start)
+
+    lane = lax.broadcasted_iota(jnp.int32, (SUB, LANES), 1)
+    sub = lax.broadcasted_iota(jnp.int32, (SUB, LANES), 0)
+    high_lane, low_lane = lane // SUB, lane % SUB
+    to_left = jnp.where(high_lane > 0, lane - SUB, jnp.where(low_lane > 0, 119 + low_lane, 0))
+    to_right = jnp.where(
+        high_lane < 15, lane + SUB, jnp.where(low_lane < 7, low_lane + 1, LANES - 1)
+    )
+    not_first_lane = lane > 0
+    not_last_lane = lane < LANES - 1
+    not_first_sub = sub > 0
+    not_last_sub = sub < SUB - 1
+
+    entry = entry_ref[chain, place]
+    angle = pulsation_ref[entry] * jnp.broadcast_to(slowness_ref[...], (SUB, LANES))
+    cosine, sine = jnp.cos(angle), jnp.sin(angle)
+    for k in range(ORDER + 1):
+        fr, fi = (
+            jnp.broadcast_to(weight_ref[entry, k, pl.ds(c, 1), :], (SUB, LANES))
+            for c in range(2)
+        )
+        turned = (fr * cosine - fi * sine, fr * sine + fi * cosine)
+        for c in range(2):
+            for part in range(NBIN // SUB):
+                spread_table[part, (ORDER + 1) * c + k] = lane_pick(
+                    turned[c], sub + part * SUB
+                )
+
+    pl.semaphore_wait(barrier, 3 * lateral - 1)
+
+    def wave_copy(f):
+        return remote(
+            wave_ref.at[f],
+            wave_in.at[slab],
+            wave_sems,
+            (f,),
+            device(worker(home, f)),
+            (slab,),
+        )
+
+    def wave_arrival(d):
+        return remote(
+            wave_ref.at[0], wave_in.at[d], wave_sems, (d,), device(owner(chain, d))
+        )
+
+    def map_copy(tick, y):
+        to = worker(home if tick == 0 else section, 2 * y + core)
+        copy = remote(
+            map_ref,
+            map_in.at[tick, slab],
+            map_sems,
+            (tick, y),
+            device(to),
+            (tick, slab // 2),
+        )
+        live = to != me
+        return copy, live if tick == 0 else live & is_deep
+
+    def map_arrival(tick, h):
+        d = core + 2 * h
+        source = owner(chain + tick, d)
+        copy = remote(map_ref, map_in.at[tick, d], map_sems, (tick, h), device(source))
+        return copy, source != me
+
+    def map_relay(tick, h):
+        part = map_in.at[tick, core + 2 * h]
+        return remote(part, part, relay_sems, (tick, h), partner)
+
+    def pass_map_on(tick):
+        for h in range(2):
+            copy, foreign = map_arrival(tick, h)
+            pl.when(foreign)(copy.wait_recv)
+            pl.when(jnp.logical_not(foreign))(own_map.wait)
+            map_relay(tick, h).start()
+
+    def start_map(tick):
+        for y in range(2):
+            copy, live = map_copy(tick, y)
+            pl.when(live)(copy.start)
+
+    start_map(0)
+    for i in range(lateral):
+        f = lax.rem(i + half * (1 - side), lateral)
+        pl.when(worker(home, f) != me)(wave_copy(f).start)
+    start_map(1)
+
+    def cell(m, r):
+        return pl.ds((m * SUB + r) * SUB, SUB)
+
+    def column(m, slot):
+        return pl.ds(m * SUB * SUB + slot, SUB, stride=SUB)
+
+    def gather_back(source, d, g):
+        return transposed([source[column(m, groups * d + g), :] for m in range(SUB)])
+
+    def tile(g, j):
+        return pl.ds(g * SUB, SUB), pl.ds(j * LANES, LANES)
+
+    def spread(load, ref, d):
+        for g in range(groups):
+            for m, x in enumerate(transposed([load(*tile(g, j)) for j in range(SUB)])):
+                ref[column(m, groups * d + g), :] = x
+
+    def fill(tick, level):
+        for d in range(lateral):
+            spread(lambda row, col: map_in[tick, d, level, row, col], bins, d)
+        n_cells = 2
+
+        def some(i, carry):
+            for n in range(n_cells):
+                where = pl.ds(pl.multiple_of((i * n_cells + n) * SUB, SUB), SUB)
+                bin_ = bins[where, :]
+                high = bin_ >= SUB
+                low_bits = bin_ % SUB
+                for row in range(ROWS):
+                    a, b = (
+                        jnp.take_along_axis(
+                            spread_table[part, row],
+                            low_bits,
+                            axis=0,
+                            mode="promise_in_bounds",
+                            wrap_negative_indices=False,
+                        )
+                        for part in range(NBIN // SUB)
+                    )
+                    coeffs[tick, level, row, where, :] = jnp.where(high, b, a)
+            return carry
+
+        lax.fori_loop(0, SUB * SUB // n_cells, some, 0)
+
+    def stencil(present, target, first=False, last=False):
+        def channel(c, carry):
+            below = []
+            for m in range(8):
+                edge = pltpu.roll(present[c, cell(m, 7), :], 1, 0)
+                edge = jnp.where(not_first_sub, edge, 0.0)
+                below.append(edge + present[c, cell(m, 0), :])
+            for r in range(8):
+                u = []
+                for m in range(8):
+                    here = present[c, cell(m, r), :]
+                    if r < 7:
+                        above = present[c, cell(m, r + 1), :]
+                    else:
+                        above = pltpu.roll(present[c, cell(m, 0), :], SUB - 1, 0)
+                        above = jnp.where(not_last_sub, above, 0.0)
+                    q = here + above
+                    u.append(below[m] + q)
+                    below[m] = q
+                left = jnp.where(not_first_lane, lane_pick(u[7], to_left), 0.0)
+                right = jnp.where(not_last_lane, lane_pick(u[0], to_right), 0.0)
+                u = [left] + u + [right]
+                h = [u[m] + u[m + 1] for m in range(9)]
+                for m in range(8):
+                    w = h[m] + h[m + 1]
+                    here = present[c, cell(m, r), :]
+                    if first:
+                        both = 0.125 * w
+                    else:
+                        both = 0.25 * w - paired_sum[c, cell(m, r), :]
+                    if not last:
+                        paired_sum[c, cell(m, r), :] = both
+                    target[c, cell(m, r), :] = both - here
+            return carry
+
+        lax.fori_loop(0, 2, channel, 0)
+
+    def add_orders(tick, level, terms, where, total):
+        re, im = (None, None) if total is None else total
+        for order, ref in terms:
+            tr, ti = (ref[c, where, :] for c in range(2))
+            br = coeffs[tick, level, order, where, :]
+            bi = coeffs[tick, level, ORDER + 1 + order, where, :]
+            dr = br * tr - bi * ti
+            di = br * ti + bi * tr
+            re, im = (dr, di) if re is None else (re + dr, im + di)
+        return re, im
+
+    def sum_so_far(where):
+        return [running[c, where, :] for c in range(2)]
+
+    def unit(tick, level, output):
+        start = starts.at[tick * LEVELS + level]
+        stencil(start, odd, first=True)
+        for i in range(SUB * SUB):
+            where = pl.ds(i * SUB, SUB)
+            total = add_orders(tick, level, [(0, start), (1, odd)], where, None)
+            for c in range(2):
+                running[c, where, :] = total[c]
+
+        def steps(i, carry):
+            stencil(odd, even)
+            stencil(even, odd)
+            for n in range(SUB * SUB):
+                where = pl.ds(n * SUB, SUB)
+                terms = [(2 * i + 2, even), (2 * i + 3, odd)]
+                total = add_orders(tick, level, terms, where, sum_so_far(where))
+                for c in range(2):
+                    running[c, where, :] = total[c]
+            return carry
+
+        lax.fori_loop(0, ORDER // 2 - 1, steps, 0)
+        stencil(odd, even, last=True)
+        for i in range(SUB * SUB):
+            where = pl.ds(i * SUB, SUB)
+            total = add_orders(tick, level, [(ORDER, even)], where, sum_so_far(where))
+            for c in range(2):
+                output[c, where, :] = total[c]
+            raw[tick, level, where, :] = total[0]
+
+    def raw_copy(tick, level, d):
+        to = owner(chain + tick, d)
+        copy = remote(
+            raw_out.at[tick, level, d],
+            raw_in.at[tick, level, place],
+            raw_sems,
+            (tick, level, d),
+            device(to),
+            (tick, level, place),
+        )
+        return copy, to != me
+
+    def own_raw(tick, level):
+        return pltpu.make_async_copy(
+            raw_out.at[tick, level, slab],
+            raw_in.at[tick, level, place],
+            own_raw_sems.at[tick, level],
+        )
+
+    def raw_arrival(tick, level, f):
+        source = worker(home if tick == 0 else section, f)
+        copy = remote(
+            raw_out.at[tick, level, f],
+            raw_in.at[tick, level, f],
+            raw_sems,
+            (tick, level, f),
+            device(source),
+        )
+        return copy, source != me
+
+    def send_raw(tick, level):
+        for d in range(lateral):
+            for g in range(groups):
+                for j, x in enumerate(gather_back(raw.at[tick, level], d, g)):
+                    raw_out[(tick, level, d) + tile(g, j)] = x
+            copy, foreign = raw_copy(tick, level, d)
+            pl.when(foreign)(copy.start)
+            pl.when(jnp.logical_not(foreign))(own_raw(tick, level).start)
+
+    def wave_back(which, d):
+        to = owner(chain + which, d)
+        copy = remote(
+            wave_out.at[which, d],
+            handed_ref.at[place],
+            fin_sems,
+            (which, d),
+            device(to),
+            (1, place),
+        )
+        return copy, to != me
+
+    def own_back(which):
+        return pltpu.make_async_copy(
+            wave_out.at[which, slab], handed_ref.at[place], own_sems.at[0]
+        )
+
+    def handed_arrival(f):
+        source = worker(jnp.maximum(section, 1), f)
+        copy = remote(
+            wave_out.at[1, f], handed_ref.at[f], fin_sems, (1, f), device(source)
+        )
+        return copy, source != me
+
+    def send_wave(which, source):
+        for d in range(lateral):
+            for c in range(2):
+                for g in range(groups):
+                    for j, x in enumerate(gather_back(source.at[c], d, g)):
+                        wave_out[(which, d, c) + tile(g, j)] = x
+            copy, foreign = wave_back(which, d)
+            pl.when(foreign)(copy.start)
+            pl.when(jnp.logical_not(foreign))(own_back(which).start)
+
+    pass_map_on(0)
+    for h in range(2):
+        map_relay(0, h).wait_recv()
+    fill(0, 0)
+    fill(0, 1)
+    for d in range(lateral):
+        foreign = owner(chain, d) != me
+        pl.when(foreign)(wave_arrival(d).wait_recv)
+        pl.when(jnp.logical_not(foreign))(own_wave.wait)
+        for c in range(2):
+            spread(lambda row, col: wave_in[d, c, row, col], starts.at[0, c], d)
+    unit(0, 0, starts.at[1])
+    pl.when(has_next)(lambda: pass_map_on(1))
+    unit(0, 1, starts.at[2])
+
+    @pl.when(chain == 0)
+    def _():
+        send_wave(0, starts.at[2])
+
+    for level in range(LEVELS):
+        send_raw(0, level)
+
+    @pl.when(has_next)
+    def _():
+        for h in range(2):
+            map_relay(1, h).wait_recv()
+        fill(1, 0)
+        fill(1, 1)
+        unit(1, 0, starts.at[3])
+        send_raw(1, 0)
+        unit(1, 1, last)
+        send_raw(1, 1)
+        send_wave(1, last)
+
+    for level in range(LEVELS):
+        for tick in range(TICKS):
+            for f in range(lateral):
+                copy, foreign = raw_arrival(tick, level, f)
+                own = jnp.logical_not(foreign)
+                if tick == 1:
+                    foreign, own = foreign & is_deep, own & is_deep
+                pl.when(foreign)(copy.wait_recv)
+                pl.when(own)(own_raw(tick, level).wait)
+        total = jnp.zeros((SUB, LANES), jnp.float32)
+        for g in range(groups):
+            for j in range(SUB):
+                value = second = None
+                for f in range(lateral):
+                    a, b = (raw_in[(t, level, f) + tile(g, j)] for t in range(TICKS))
+                    value = a if value is None else value + a
+                    second = b if second is None else second + b
+                value = value + jnp.where(is_deep, second, 0.0)
+                image_ref[(level,) + tile(g, j)] = value
+                total = total + value * value
+        sum_own[pl.ds(level * SUB, SUB), :] = total
+
+    def sum_copy(x):
+        mate = lax.rem(slab + x, lateral)
+        return remote(sum_own, sum_in.at[x], sum_sems, (x,), device(owner(section, mate)))
+
+    for x in range(1, lateral):
+        sum_copy(x).start()
+    total = sum_own[...]
+    for x in range(1, lateral):
+        sum_copy(x).wait_recv()
+        total = total + sum_in[x]
+    cells = length * lateral * SUB * LANES
+    for level in range(LEVELS):
+        mean = (
+            jnp.sum(total[level * SUB : (level + 1) * SUB], axis=(0, 1), keepdims=True) / cells
+        )
+        scale = jnp.broadcast_to(1.0 / jnp.sqrt(mean + 1e-06), (SUB, LANES))
+        for g in range(groups):
+            for j in range(SUB):
+                where = (level,) + tile(g, j)
+                image_ref[where] = image_ref[where] * scale
+    for f in range(lateral):
+        copy, foreign = handed_arrival(f)
+        pl.when(foreign)(copy.wait_recv)
+        pl.when(jnp.logical_not(foreign))(own_back(0).wait)
+    for x in range(1, lateral):
+        sum_copy(x).wait_send()
+    for tick in range(TICKS):
+        for y in range(2):
+            copy, live = map_copy(tick, y)
+            pl.when(live)(copy.wait_send)
+    for h in range(2):
+        map_relay(0, h).wait_send()
+        pl.when(has_next)(map_relay(1, h).wait_send)
+    for n in range(lateral):
+        pl.when(worker(home, n) != me)(wave_copy(n).wait_send)
+        for which, live in ((0, chain == 0), (1, has_next)):
+            copy, foreign = wave_back(which, n)
+            pl.when(foreign & live)(copy.wait_send)
+        for level in range(LEVELS):
+            for tick in range(TICKS):
+                copy, foreign = raw_copy(tick, level, n)
+                pl.when(foreign if tick == 0 else foreign & has_next)(copy.wait_send)
+
+
+def phase_table(filter_weights, scaled_pulsations, inverse_speed_classes):
+    angle = scaled_pulsations[:, None] * inverse_speed_classes[None, :]
+    cosine = jnp.cos(angle)[:, None, :]
+    sine = jnp.sin(angle)[:, None, :]
+    by_order = jnp.transpose(filter_weights, (2, 0, 3, 1))
+    real = by_order[0] * cosine - by_order[1] * sine
+    imag = by_order[0] * sine + by_order[1] * cosine
+    table = jnp.stack([real, imag], axis=2).reshape(NW, 2 * (ORDER + 1), NBIN)
+    return jnp.pad(table, ((0, 0), (0, 0), (0, LANES - NBIN)))
+
+
+def chains(
+    incoming_wave,
+    speed_class_map,
+    spectral_entry_index,
+    filter_weights,
+    scaled_pulsations,
+    inverse_speed_classes,
+):
+    count = lax.axis_size("strip")
+    lateral = count // SECTIONS
+    length, across = incoming_wave.shape[2:]
+    tall = length * lateral * SUB
+    f32 = jnp.float32
+    vmem = pl.BlockSpec(memory_space=pltpu.VMEM)
+    smem = pl.BlockSpec(memory_space=pltpu.SMEM)
+    anywhere = pl.BlockSpec(memory_space=pl.ANY)
+    blank = LANES - NBIN
+    weights = jnp.pad(
+        jnp.transpose(filter_weights, (0, 3, 2, 1)), ((0, 0), (0, 0), (0, 0), (0, blank))
+    )
+    slowness = jnp.pad(inverse_speed_classes[None], ((0, 0), (0, blank)))
+
+    def dma(*shape):
+        return pltpu.SemaphoreType.DMA((2,) + shape)
+
+    return pl.pallas_call(
+        functools.partial(chain_kernel, count),
+        out_shape=(
+            jax.ShapeDtypeStruct(speed_class_map.shape, f32),
+            jax.ShapeDtypeStruct(incoming_wave.shape, f32),
+        ),
+        in_specs=[smem, smem, vmem, vmem, anywhere, anywhere],
+        out_specs=(vmem, vmem),
+        scratch_shapes=[
+            pltpu.VMEM((TICKS * LEVELS, 2, tall, LANES), f32),
+            pltpu.VMEM((2, tall, LANES), f32),
+            pltpu.VMEM((2, tall, LANES), f32),
+            pltpu.VMEM((2, tall, LANES), f32),
+            pltpu.VMEM((2, tall, LANES), f32),
+            pltpu.VMEM((2, tall, LANES), f32),
+            pltpu.VMEM((TICKS, LEVELS, ROWS, tall, LANES), f32),
+            pltpu.VMEM((NBIN // SUB, ROWS, SUB, LANES), f32),
+            pltpu.VMEM((lateral, 2, length, across), f32),
+            pltpu.VMEM((TICKS, lateral, LEVELS, length, across), jnp.int32),
+            pltpu.VMEM((tall, LANES), jnp.int32),
+            pltpu.VMEM((TICKS, LEVELS, tall, LANES), f32),
+            pltpu.VMEM((2, lateral, 2, length, across), f32),
+            pltpu.VMEM((TICKS, LEVELS, lateral, length, across), f32),
+            pltpu.VMEM((TICKS, LEVELS, lateral, length, across), f32),
+            pltpu.VMEM((LEVELS * SUB, LANES), f32),
+            pltpu.VMEM((lateral, LEVELS * SUB, LANES), f32),
+            dma(lateral),
+            dma(TICKS, 2),
+            dma(TICKS, 2),
+            dma(2, lateral),
+            dma(TICKS, LEVELS, lateral),
+            dma(lateral),
+            pltpu.SemaphoreType.DMA((2,)),
+            pltpu.SemaphoreType.DMA((TICKS, LEVELS)),
+        ],
+        compiler_params=pltpu.CompilerParams(
+            collective_id=0, has_side_effects=True, vmem_limit_bytes=60 * 1024 * 1024
+        ),
+    )(
+        spectral_entry_index,
+        scaled_pulsations,
+        slowness,
+        weights,
+        incoming_wave,
+        speed_class_map,
+    )
+
+
 def fits(mesh):
     lateral = mesh.shape["strip"] // SECTIONS
     return NFREQ % 2 == 0 and lateral % 4 == 0
 
 
+def whole_section(mesh, wave):
+    lateral = mesh.shape["strip"] // SECTIONS
+    full = lateral * wave.shape[2] == SUB * SUB and wave.shape[3] == SUB * LANES
+    return lateral == NFREQ == 4 and wave.shape[2] % SUB == 0 and full
+
+
 def body_for(mesh):
     def body(wave, *rest):
         whole = wave.shape[3] == SUB * LANES and wave.shape[2] % SUB == 0
+        if whole_section(mesh, wave):
+            return chains(wave, *rest)
         if fits(mesh) and whole and wave.shape[2] >= ORDER:
             return paired(wave, *rest)
         return shards(wave, *rest)

time: 102 us -> 65.9 us (0.65)
  the two profiles are of different devices: /device:TPU:1 before, /device:TPU:9 now
where the time goes in v3:
time: 65.9 us; the launch traced here: 65.6 us
  Pallas kernels  58.7 us (89%)
  local copies, waits for them, and re-layouts  6.3 us (10%)
    pallas_call x1, Pallas kernels, chains(): pl.pallas_call(functools.partial(chain_kernel, count), out_shape=(jax.Sha...  58.7 us
    unnamed x4, local copies, waits for them, and re-layouts  4.1 us
    pad x1, local copies, waits for them, and re-layouts, chains(): jnp.pad(jnp.transpose(filter_weights, (0, 3, 2, 1)), ((0, 0), (0, 0), (0,...  1.69 us

profile of v3, /device:TPU:9, one launch (start us, length us, event | category | flops | bytes accessed | tf_op | source)
XLA Modules:
  0.0 65.6 jit_solution(18436969367759531872)
XLA Ops:
  0.6 0.0 copy-start
  0.6 0.6 copy-done
  1.3 0.5 pad.8.slowness_ref
  1.8 1.7 %pad.9.weight_ref = f32[16,13,2,128]{3,2,1,0:T(2,128)} pad(f32[16,13,2,16]{3,2,1,0:T(2,128)} %bitcast.2, f32[]{:T(128)} %constant.2.clone.1), padding=0_0x0_0x0_0x0_112 | pad | bytes 239620 | tf_op jit(solution)/shard_map/jit(_pad)/pad | solution.py:1176
  3.5 58.7 %shard_map.77 = (f32[2,16,1024]{2,1,0:T(8,128)}, f32[4,2,16,1024]{3,2,1,0:T(8,128)}) custom-call(s32[4,4]{1,0:T(4,128)} %entry_ref.1, f32[16]{0:T(128)} %pulsation_ref.1, f32[1,128]{1,0:T(1,128)} %pad.8.slowness_ref, f32[16,13,2,128]{3,2,1,0:T(2,128)} %pad.9.weight_ref, f32[4,2,16,1024]{3,2,1,0:T(8,128)} %wave_ref.1, s32[2,16,1024]{2,1,0:T(8,128)} %map_ref.1), custom_call_target="tpu_custom_call" | custom-call | tf_op jit(solution)/shard_map/pallas_call | solution.py:1184
  62.2 1.6 %copy.10 = f32[2,16,1024]{2,1,0:T(8,128)} copy(f32[2,16,1024]{2,1,0:T(8,128)} %get-tuple-element.4) | data formatting | bytes 262144
  63.7 1.9 %copy.11 = f32[4,2,16,1024]{3,2,1,0:T(8,128)} copy(f32[4,2,16,1024]{3,2,1,0:T(8,128)} %get-tuple-element.5) | data formatting | bytes 1048576
Async XLA Ops:
  0.6 0.7 copy-start

commit v4 on v3

--- a/solution.py
+++ b/solution.py
@@ -682,6 +682,12 @@
     map_ref,
     image_ref,
     handed_ref,
+    entries,
+    pulsations,
+    slownesses,
+    weights,
+    rows,
+    hop,
     starts,
     last,
     even,
@@ -699,7 +705,9 @@
     raw_in,
     sum_own,
     sum_in,
+    small_sems,
     wave_sems,
+    hop_sems,
     map_sems,
     relay_sems,
     fin_sems,
@@ -758,6 +766,19 @@
         def _():
             pl.semaphore_signal(barrier, inc=1, device_id=device(mate), device_id_type=MESH)
 
+    small = [
+        pltpu.make_async_copy(source, target, small_sems.at[n])
+        for n, (source, target) in enumerate(
+            (
+                (entry_ref, entries),
+                (pulsation_ref, pulsations),
+                (slowness_ref, slownesses),
+                (weight_ref, weights),
+            )
+        )
+    ]
+    for copy in small:
+        copy.start()
     own_wave = pltpu.make_async_copy(wave_ref.at[place], wave_in.at[slab], own_sems.at[0])
     own_map = pltpu.make_async_copy(map_ref, map_in.at[side, slab], own_sems.at[1])
     pl.when(near)(own_wave.start)
@@ -775,21 +796,6 @@
     not_first_sub = sub > 0
     not_last_sub = sub < SUB - 1
 
-    entry = entry_ref[chain, place]
-    angle = pulsation_ref[entry] * jnp.broadcast_to(slowness_ref[...], (SUB, LANES))
-    cosine, sine = jnp.cos(angle), jnp.sin(angle)
-    for k in range(ORDER + 1):
-        fr, fi = (
-            jnp.broadcast_to(weight_ref[entry, k, pl.ds(c, 1), :], (SUB, LANES))
-            for c in range(2)
-        )
-        turned = (fr * cosine - fi * sine, fr * sine + fi * cosine)
-        for c in range(2):
-            for part in range(NBIN // SUB):
-                spread_table[part, (ORDER + 1) * c + k] = lane_pick(
-                    turned[c], sub + part * SUB
-                )
-
     pl.semaphore_wait(barrier, 3 * lateral - 1)
 
     def wave_copy(f):
@@ -842,11 +848,57 @@
             copy, live = map_copy(tick, y)
             pl.when(live)(copy.start)
 
+    far = side == 1
+
+    def hop_in(f):
+        return pltpu.make_async_remote_copy(
+            src_ref=wave_ref.at[f],
+            dst_ref=hop.at[f],
+            send_sem=wave_sems.at[0, f],
+            recv_sem=hop_sems.at[1, f],
+            device_id=device(worker(plane, core)),
+            device_id_type=MESH,
+        )
+
+    def hop_on(f):
+        return pltpu.make_async_remote_copy(
+            src_ref=hop.at[f],
+            dst_ref=wave_in.at[core],
+            send_sem=hop_sems.at[0, f],
+            recv_sem=wave_sems.at[1, core],
+            device_id=device(worker(plane + 1, f)),
+            device_id_type=MESH,
+        )
+
     start_map(0)
-    for i in range(lateral):
-        f = lax.rem(i + half * (1 - side), lateral)
-        pl.when(worker(home, f) != me)(wave_copy(f).start)
+    for f in range(half):
+        pl.when(far)(hop_in(f).start)
+    for f in range(half, lateral):
+        wave_copy(f).start()
+    for f in range(half):
+        pl.when(near & (worker(home, f) != me))(wave_copy(f).start)
     start_map(1)
+
+    for copy in small:
+        copy.wait()
+    entry = entries[chain, place]
+    angle = pulsations[entry] * slownesses[...]
+    cosine, sine = jnp.cos(angle), jnp.sin(angle)
+    for k in range(ORDER + 1):
+        fr, fi = (weights[entry, k, pl.ds(c, 1), :] for c in range(2))
+        rows[pl.ds(k, 1), pl.ds(0, NBIN)] = fr * cosine - fi * sine
+        rows[pl.ds(ORDER + 1 + k, 1), pl.ds(0, NBIN)] = fr * sine + fi * cosine
+    for n in range(ROWS):
+        row = jnp.broadcast_to(rows[pl.ds(n, 1), :], (SUB, LANES))
+        for part in range(NBIN // SUB):
+            spread_table[part, n] = lane_pick(row, sub + part * SUB)
+
+    @pl.when(near)
+    def _():
+        for f in range(half):
+            hop_in(f).wait_recv()
+            hop_on(f).start()
+
 
     def cell(m, r):
         return pl.ds((m * SUB + r) * SUB, SUB)
@@ -887,7 +939,7 @@
                         )
                         for part in range(NBIN // SUB)
                     )
-                    coeffs[tick, level, row, where, :] = jnp.where(high, b, a)
+                    coeffs[level, row, where, :] = jnp.where(high, b, a)
             return carry
 
         lax.fori_loop(0, SUB * SUB // n_cells, some, 0)
@@ -933,8 +985,8 @@
         re, im = (None, None) if total is None else total
         for order, ref in terms:
             tr, ti = (ref[c, where, :] for c in range(2))
-            br = coeffs[tick, level, order, where, :]
-            bi = coeffs[tick, level, ORDER + 1 + order, where, :]
+            br = coeffs[level, order, where, :]
+            bi = coeffs[level, ORDER + 1 + order, where, :]
             dr = br * tr - bi * ti
             di = br * ti + bi * tr
             re, im = (dr, di) if re is None else (re + dr, im + di)
@@ -1050,22 +1102,25 @@
         map_relay(0, h).wait_recv()
     fill(0, 0)
     fill(0, 1)
-    for d in range(lateral):
-        foreign = owner(chain, d) != me
-        pl.when(foreign)(wave_arrival(d).wait_recv)
-        pl.when(jnp.logical_not(foreign))(own_wave.wait)
-        for c in range(2):
-            spread(lambda row, col: wave_in[d, c, row, col], starts.at[0, c], d)
+    def take_waves(order):
+        for d in order:
+            foreign = owner(chain, d) != me
+            pl.when(foreign)(wave_arrival(d).wait_recv)
+            pl.when(jnp.logical_not(foreign))(own_wave.wait)
+            for c in range(2):
+                spread(lambda row, col: wave_in[d, c, row, col], starts.at[0, c], d)
+
+    pl.when(near)(lambda: take_waves((2, 3, 0, 1)))
+    pl.when(far)(lambda: take_waves((0, 1, 2, 3)))
     unit(0, 0, starts.at[1])
     pl.when(has_next)(lambda: pass_map_on(1))
+    send_raw(0, 0)
     unit(0, 1, starts.at[2])
+    send_raw(0, 1)
 
     @pl.when(chain == 0)
     def _():
         send_wave(0, starts.at[2])
-
-    for level in range(LEVELS):
-        send_raw(0, level)
 
     @pl.when(has_next)
     def _():
@@ -1136,6 +1191,8 @@
         pl.when(has_next)(map_relay(1, h).wait_send)
     for n in range(lateral):
         pl.when(worker(home, n) != me)(wave_copy(n).wait_send)
+        if n < half:
+            pl.when(near)(hop_on(n).wait_send)
         for which, live in ((0, chain == 0), (1, has_next)):
             copy, foreign = wave_back(which, n)
             pl.when(foreign & live)(copy.wait_send)
@@ -1170,14 +1227,7 @@
     tall = length * lateral * SUB
     f32 = jnp.float32
     vmem = pl.BlockSpec(memory_space=pltpu.VMEM)
-    smem = pl.BlockSpec(memory_space=pltpu.SMEM)
-    anywhere = pl.BlockSpec(memory_space=pl.ANY)
-    blank = LANES - NBIN
-    weights = jnp.pad(
-        jnp.transpose(filter_weights, (0, 3, 2, 1)), ((0, 0), (0, 0), (0, 0), (0, blank))
-    )
-    slowness = jnp.pad(inverse_speed_classes[None], ((0, 0), (0, blank)))
-
+    anywhere = pl.BlockSpec(memory_space=pltpu.HBM)
     def dma(*shape):
         return pltpu.SemaphoreType.DMA((2,) + shape)
 
@@ -1187,16 +1237,22 @@
             jax.ShapeDtypeStruct(speed_class_map.shape, f32),
             jax.ShapeDtypeStruct(incoming_wave.shape, f32),
         ),
-        in_specs=[smem, smem, vmem, vmem, anywhere, anywhere],
+        in_specs=[anywhere] * 6,
         out_specs=(vmem, vmem),
         scratch_shapes=[
+            pltpu.SMEM(spectral_entry_index.shape, jnp.int32),
+            pltpu.SMEM((NW,), f32),
+            pltpu.VMEM((1, NBIN), f32),
+            pltpu.VMEM((NW, ORDER + 1, 2, NBIN), f32),
+            pltpu.VMEM((ROWS, LANES), f32),
+            pltpu.VMEM((lateral // 2, 2, length, across), f32),
             pltpu.VMEM((TICKS * LEVELS, 2, tall, LANES), f32),
             pltpu.VMEM((2, tall, LANES), f32),
             pltpu.VMEM((2, tall, LANES), f32),
             pltpu.VMEM((2, tall, LANES), f32),
             pltpu.VMEM((2, tall, LANES), f32),
             pltpu.VMEM((2, tall, LANES), f32),
-            pltpu.VMEM((TICKS, LEVELS, ROWS, tall, LANES), f32),
+            pltpu.VMEM((LEVELS, ROWS, tall, LANES), f32),
             pltpu.VMEM((NBIN // SUB, ROWS, SUB, LANES), f32),
             pltpu.VMEM((lateral, 2, length, across), f32),
             pltpu.VMEM((TICKS, lateral, LEVELS, length, across), jnp.int32),
@@ -1207,7 +1263,9 @@
             pltpu.VMEM((TICKS, LEVELS, lateral, length, across), f32),
             pltpu.VMEM((LEVELS * SUB, LANES), f32),
             pltpu.VMEM((lateral, LEVELS * SUB, LANES), f32),
+            pltpu.SemaphoreType.DMA((4,)),
             dma(lateral),
+            dma(lateral // 2),
             dma(TICKS, 2),
             dma(TICKS, 2),
             dma(2, lateral),
@@ -1217,13 +1275,13 @@
             pltpu.SemaphoreType.DMA((TICKS, LEVELS)),
         ],
         compiler_params=pltpu.CompilerParams(
-            collective_id=0, has_side_effects=True, vmem_limit_bytes=60 * 1024 * 1024
+            collective_id=0, has_side_effects=True, vmem_limit_bytes=32 * 1024 * 1024
         ),
     )(
         spectral_entry_index,
         scaled_pulsations,
-        slowness,
-        weights,
+        inverse_speed_classes[None],
+        jnp.transpose(filter_weights, (0, 3, 2, 1)),
         incoming_wave,
         speed_class_map,
     )

time: 65.9 us -> 56.1 us (0.85)
  the two profiles are of different devices: /device:TPU:9 before, /device:TPU:1 now
where the time goes in v4:
time: 56.1 us; the launch traced here: 55.9 us
  Pallas kernels  50.2 us (89%)
  local copies, waits for them, and re-layouts  4.99 us (9%)
  between operations  0.67 us (1%)
    pallas_call x1, Pallas kernels, chains(): pl.pallas_call(functools.partial(chain_kernel, count), out_shape=(jax.Sha...  50.2 us
    unnamed x14, local copies, waits for them, and re-layouts  4.99 us

profile of v4, /device:TPU:1, one launch (start us, length us, event | category | flops | bytes accessed | tf_op | source)
XLA Modules:
  0.0 55.9 jit_solution(5094924512933223200)
XLA Ops:
  0.6 0.0 copy-start.3
  0.6 0.0 copy-start.4
  0.7 0.0 copy-start.5
  0.7 0.7 %copy-done.3 = s32[4,4]{1,0:T(4,128)S(1)} copy-done((s32[4,4]{1,0:T(4,128)S(1)}, s32[4,4]{1,0:T(4,128)}, u32[]{:S(2)}) %copy-start.3) | copy-done | bytes 88
  1.3 0.0 copy-done.4
  1.3 0.0 copy-done.5
  1.3 0.0 copy-start
  1.3 1.0 %copy-done = f32[4,2,16,1024]{3,2,1,0:T(8,128)S(1)} copy-done((f32[4,2,16,1024]{3,2,1,0:T(8,128)S(1)}, f32[4,2,16,1024]{3,2,1,0:T(8,128)}, u32[]{:S(2)}) %copy-start) | copy-done | bytes 524312
  2.4 0.0 copy-start.1
  2.4 0.9 %copy-done.1 = f32[16,16,2,13]{1,2,3,0:T(2,128)S(1)} copy-done((f32[16,16,2,13]{1,2,3,0:T(2,128)S(1)}, f32[16,16,2,13]{1,2,3,0:T(2,128)}, u32[]{:S(2)}) %copy-start.1) | copy-done | bytes 26648
  3.3 0.0 copy-start.2
  3.3 0.9 %copy-done.2 = s32[2,16,1024]{2,1,0:T(8,128)S(1)} copy-done((s32[2,16,1024]{2,1,0:T(8,128)S(1)}, s32[2,16,1024]{2,1,0:T(8,128)}, u32[]{:S(2)}) %copy-start.2) | copy-done | bytes 131096
  4.2 50.2 %shard_map.77 = (f32[2,16,1024]{2,1,0:T(8,128)S(1)}, f32[4,2,16,1024]{3,2,1,0:T(8,128)S(1)}) custom-call(s32[4,4]{1,0:T(4,128)S(1)} %copy-done.3, f32[16]{0:T(128)S(1)} %copy-done.4, f32[1,16]{1,0:T(1,128)S(1)} %bitcast.3, f32[16,13,2,16]{3,2,1,0:T(2,128)S(1)} %bitcast.2, f32[4,2,16,1024]{3,2,1,0:T(8,128)S(1)} %copy-done, s32[2,16,1024]{2,1,0:T(8,128)S(1)} %copy-done.2), custom_call_target="tpu_custom_call" | custom-call | tf_op jit(solution)/shard_map/pallas_call | solution.py:1234
  54.4 0.7 %copy.10 = f32[2,16,1024]{2,1,0:T(8,128)} copy(f32[2,16,1024]{2,1,0:T(8,128)S(1)} %get-tuple-element.4) | data formatting | bytes 262144
  55.1 0.8 %copy.11 = f32[4,2,16,1024]{3,2,1,0:T(8,128)} copy(f32[4,2,16,1024]{3,2,1,0:T(8,128)S(1)} %get-tuple-element.5) | data formatting | bytes 1048576
Async XLA Ops:
  0.6 0.7 %copy-start.3 = (s32[4,4]{1,0:T(4,128)S(1)}, s32[4,4]{1,0:T(4,128)}, u32[]{:S(2)}) copy-start(s32[4,4]{1,0:T(4,128)} %entry_ref.1) | copy-start | bytes 196
  0.6 0.7 %copy-start.4 = (f32[16]{0:T(128)S(1)}, f32[16]{0:T(128)}, u32[]{:S(2)}) copy-start(f32[16]{0:T(128)} %pulsation_ref.1) | copy-start | bytes 196
  0.7 0.7 %copy-start.5 = (f32[16]{0:T(128)S(1)}, f32[16]{0:T(128)}, u32[]{:S(2)}) copy-start(f32[16]{0:T(128)} %param.11) | copy-start | bytes 196
  1.3 1.0 %copy-start = (f32[4,2,16,1024]{3,2,1,0:T(8,128)S(1)}, f32[4,2,16,1024]{3,2,1,0:T(8,128)}, u32[]{:S(2)}) copy-start(f32[4,2,16,1024]{3,2,1,0:T(8,128)} %wave_ref.1) | copy-start | bytes 1572868
  2.4 0.9 %copy-start.1 = (f32[16,16,2,13]{1,2,3,0:T(2,128)S(1)}, f32[16,16,2,13]{1,2,3,0:T(2,128)}, u32[]{:S(2)}) copy-start(f32[16,16,2,13]{1,2,3,0:T(2,128)} %param.9) | copy-start | bytes 79876
  3.3 0.9 %copy-start.2 = (s32[2,16,1024]{2,1,0:T(8,128)S(1)}, s32[2,16,1024]{2,1,0:T(8,128)}, u32[]{:S(2)}) copy-start(s32[2,16,1024]{2,1,0:T(8,128)} %map_ref.1) | copy-start | bytes 393220

commit v5 on v4

--- a/solution.py
+++ b/solution.py
@@ -708,6 +708,7 @@
     small_sems,
     wave_sems,
     hop_sems,
+    on_sems,
     map_sems,
     relay_sems,
     fin_sems,
@@ -844,40 +845,56 @@
             map_relay(tick, h).start()
 
     def start_map(tick):
-        for y in range(2):
+        for y in (1, 0):
             copy, live = map_copy(tick, y)
             pl.when(live)(copy.start)
 
     far = side == 1
 
-    def hop_in(f):
+    def hop_in(i):
         return pltpu.make_async_remote_copy(
-            src_ref=wave_ref.at[f],
-            dst_ref=hop.at[f],
-            send_sem=wave_sems.at[0, f],
-            recv_sem=hop_sems.at[1, f],
+            src_ref=wave_ref.at[i // 2, i % 2],
+            dst_ref=hop.at[i // 2, i % 2],
+            send_sem=hop_sems.at[0, i],
+            recv_sem=hop_sems.at[1, i],
             device_id=device(worker(plane, core)),
             device_id_type=MESH,
         )
 
-    def hop_on(f):
-        return pltpu.make_async_remote_copy(
-            src_ref=hop.at[f],
-            dst_ref=wave_in.at[core],
-            send_sem=hop_sems.at[0, f],
-            recv_sem=wave_sems.at[1, core],
-            device_id=device(worker(plane + 1, f)),
-            device_id_type=MESH,
+    def hop_on(i):
+        return remote(
+            hop.at[i // 2, i % 2],
+            wave_in.at[core, i % 2],
+            on_sems,
+            (i,),
+            device(worker(plane + 1, i // 2)),
+            (2 * core + i % 2,),
+        )
+
+    def hop_arrival(d, c):
+        return remote(
+            hop.at[0, c],
+            wave_in.at[d, c],
+            on_sems,
+            (2 * d + c,),
+            device(worker(chain, d)),
         )
 
     start_map(0)
-    for f in range(half):
-        pl.when(far)(hop_in(f).start)
+
+    @pl.when(far)
+    def _():
+        for i in range(lateral):
+            hop_in(i).start()
+
     for f in range(half, lateral):
         wave_copy(f).start()
-    for f in range(half):
-        pl.when(near & (worker(home, f) != me))(wave_copy(f).start)
-    start_map(1)
+
+    @pl.when(near)
+    def _():
+        for f in range(half):
+            pl.when(worker(home, f) != me)(wave_copy(f).start)
+        start_map(1)
 
     for copy in small:
         copy.wait()
@@ -893,11 +910,12 @@
         for part in range(NBIN // SUB):
             spread_table[part, n] = lane_pick(row, sub + part * SUB)
 
-    @pl.when(near)
-    def _():
-        for f in range(half):
-            hop_in(f).wait_recv()
-            hop_on(f).start()
+    def pass_waves_on(some):
+        for i in some:
+            hop_in(i).wait_recv()
+            hop_on(i).start()
+
+    pl.when(near)(lambda: pass_waves_on(range(lateral - 1)))
 
 
     def cell(m, r):
@@ -920,7 +938,7 @@
     def fill(tick, level):
         for d in range(lateral):
             spread(lambda row, col: map_in[tick, d, level, row, col], bins, d)
-        n_cells = 2
+        n_cells = 4
 
         def some(i, carry):
             for n in range(n_cells):
@@ -1100,7 +1118,9 @@
     pass_map_on(0)
     for h in range(2):
         map_relay(0, h).wait_recv()
+    pl.when(far)(lambda: start_map(1))
     fill(0, 0)
+    pl.when(near)(lambda: pass_waves_on((lateral - 1,)))
     fill(0, 1)
     def take_waves(order):
         for d in order:
@@ -1110,11 +1130,18 @@
             for c in range(2):
                 spread(lambda row, col: wave_in[d, c, row, col], starts.at[0, c], d)
 
-    pl.when(near)(lambda: take_waves((2, 3, 0, 1)))
+    @pl.when(near)
+    def _():
+        take_waves((2, 3))
+        for d in range(half):
+            for c in range(2):
+                hop_arrival(d, c).wait_recv()
+                spread(lambda row, col: wave_in[d, c, row, col], starts.at[0, c], d)
+
     pl.when(far)(lambda: take_waves((0, 1, 2, 3)))
     unit(0, 0, starts.at[1])
+    send_raw(0, 0)
     pl.when(has_next)(lambda: pass_map_on(1))
-    send_raw(0, 0)
     unit(0, 1, starts.at[2])
     send_raw(0, 1)
 
@@ -1162,6 +1189,27 @@
 
     for x in range(1, lateral):
         sum_copy(x).start()
+    for tick in range(TICKS):
+        for y in range(2):
+            copy, live = map_copy(tick, y)
+            pl.when(live)(copy.wait_send)
+    for h in range(2):
+        map_relay(0, h).wait_send()
+        pl.when(has_next)(map_relay(1, h).wait_send)
+    for n in range(lateral):
+        if n < half:
+            pl.when(near & (worker(home, n) != me))(wave_copy(n).wait_send)
+        else:
+            wave_copy(n).wait_send()
+        pl.when(near)(hop_on(n).wait_send)
+        pl.when(far)(hop_in(n).wait_send)
+        for which, live in ((0, chain == 0), (1, has_next)):
+            copy, foreign = wave_back(which, n)
+            pl.when(foreign & live)(copy.wait_send)
+        for level in range(LEVELS):
+            for tick in range(TICKS):
+                copy, foreign = raw_copy(tick, level, n)
+                pl.when(foreign if tick == 0 else foreign & has_next)(copy.wait_send)
     total = sum_own[...]
     for x in range(1, lateral):
         sum_copy(x).wait_recv()
@@ -1182,24 +1230,6 @@
         pl.when(jnp.logical_not(foreign))(own_back(0).wait)
     for x in range(1, lateral):
         sum_copy(x).wait_send()
-    for tick in range(TICKS):
-        for y in range(2):
-            copy, live = map_copy(tick, y)
-            pl.when(live)(copy.wait_send)
-    for h in range(2):
-        map_relay(0, h).wait_send()
-        pl.when(has_next)(map_relay(1, h).wait_send)
-    for n in range(lateral):
-        pl.when(worker(home, n) != me)(wave_copy(n).wait_send)
-        if n < half:
-            pl.when(near)(hop_on(n).wait_send)
-        for which, live in ((0, chain == 0), (1, has_next)):
-            copy, foreign = wave_back(which, n)
-            pl.when(foreign & live)(copy.wait_send)
-        for level in range(LEVELS):
-            for tick in range(TICKS):
-                copy, foreign = raw_copy(tick, level, n)
-                pl.when(foreign if tick == 0 else foreign & has_next)(copy.wait_send)
 
 
 def phase_table(filter_weights, scaled_pulsations, inverse_speed_classes):
@@ -1227,7 +1257,7 @@
     tall = length * lateral * SUB
     f32 = jnp.float32
     vmem = pl.BlockSpec(memory_space=pltpu.VMEM)
-    anywhere = pl.BlockSpec(memory_space=pltpu.HBM)
+    anywhere = pl.BlockSpec(memory_space=pl.ANY)
     def dma(*shape):
         return pltpu.SemaphoreType.DMA((2,) + shape)
 
@@ -1265,7 +1295,8 @@
             pltpu.VMEM((lateral, LEVELS * SUB, LANES), f32),
             pltpu.SemaphoreType.DMA((4,)),
             dma(lateral),
-            dma(lateral // 2),
+            dma(lateral),
+            dma(lateral),
             dma(TICKS, 2),
             dma(TICKS, 2),
             dma(2, lateral),
@@ -1278,12 +1309,17 @@
             collective_id=0, has_side_effects=True, vmem_limit_bytes=32 * 1024 * 1024
         ),
     )(
-        spectral_entry_index,
-        scaled_pulsations,
-        inverse_speed_classes[None],
-        jnp.transpose(filter_weights, (0, 3, 2, 1)),
-        incoming_wave,
-        speed_class_map,
+        *(
+            pltpu.with_memory_space_constraint(x, pltpu.HBM)
+            for x in (
+                spectral_entry_index,
+                scaled_pulsations,
+                inverse_speed_classes[None],
+                jnp.transpose(filter_weights, (0, 3, 2, 1)),
+                incoming_wave,
+                speed_class_map,
+            )
+        )
     )
 
 

time: 56.1 us -> 50.6 us (0.902)
  local copies, waits for them, and re-layouts: 4.99 us -> 1.45 us
  Pallas kernels: 50.2 us -> 48.4 us
    unnamed x14 -> x2, local copies, waits for them, and re-layouts: 4.99 us -> 1.45 us
    pallas_call x1, Pallas kernels: 50.2 us -> 48.4 us  [chains(): pl.pallas_call(functools.partial(chain_kernel, count), out_shape=(jax.Sha...]
where the time goes in v5:
time: 50.6 us; the launch traced here: 50.5 us
  Pallas kernels  48.4 us (96%)
  local copies, waits for them, and re-layouts  1.45 us (3%)
  between operations  0.64 us (1%)
    pallas_call x1, Pallas kernels, chains(): pl.pallas_call(functools.partial(chain_kernel, count), out_shape=(jax.Sha...  48.4 us
    unnamed x2, local copies, waits for them, and re-layouts  1.45 us

profile of v5, /device:TPU:1, one launch (start us, length us, event | category | flops | bytes accessed | tf_op | source)
XLA Modules:
  0.0 50.5 jit_solution(2110977437778164695)
XLA Ops:
  0.6 48.4 %shard_map.77 = (f32[2,16,1024]{2,1,0:T(8,128)S(1)}, f32[4,2,16,1024]{3,2,1,0:T(8,128)S(1)}) custom-call(s32[4,4]{1,0:T(4,128)} %entry_ref.1, f32[16]{0:T(128)} %pulsation_ref.1, f32[1,16]{1,0:T(1,128)} %bitcast.3, f32[16,13,2,16]{3,2,1,0:T(2,128)} %bitcast.2, f32[4,2,16,1024]{3,2,1,0:T(8,128)} %wave_ref.1, s32[2,16,1024]{2,1,0:T(8,128)} %map_ref.1), custom_call_target="tpu_custom_call" | custom-call | tf_op jit(solution)/shard_map/pallas_call | solution.py:1264
  49.0 0.7 %copy.10 = f32[2,16,1024]{2,1,0:T(8,128)} copy(f32[2,16,1024]{2,1,0:T(8,128)S(1)} %get-tuple-element.4) | data formatting | bytes 262144
  49.7 0.8 %copy.11 = f32[4,2,16,1024]{3,2,1,0:T(8,128)} copy(f32[4,2,16,1024]{3,2,1,0:T(8,128)S(1)} %get-tuple-element.5) | data formatting | bytes 1048576

commit v6 on v5

--- a/solution.py
+++ b/solution.py
@@ -701,7 +701,7 @@
     bins,
     raw,
     wave_out,
-    raw_out,
+    summed,
     raw_in,
     sum_own,
     sum_in,
@@ -731,6 +731,7 @@
     slab = lax.rem(place + half, lateral)
     home = lax.rem(section + 1, SECTIONS)
     near = side == 0
+    slab_home = side
     has_next = chain < SECTIONS - 1
     is_deep = section > 0
 
@@ -938,7 +939,7 @@
     def fill(tick, level):
         for d in range(lateral):
             spread(lambda row, col: map_in[tick, d, level, row, col], bins, d)
-        n_cells = 4
+        n_cells = 16
 
         def some(i, carry):
             for n in range(n_cells):
@@ -1040,12 +1041,18 @@
             total = add_orders(tick, level, [(ORDER, even)], where, sum_so_far(where))
             for c in range(2):
                 output[c, where, :] = total[c]
-            raw[tick, level, where, :] = total[0]
+            raw[tick, level, i] = total[0]
+
+    def slot(n):
+        return pl.ds(groups * n, groups)
+
+    def raw_part(tick, level, d):
+        return raw.at[tick, level, :, slot(d), :]
 
     def raw_copy(tick, level, d):
         to = owner(chain + tick, d)
         copy = remote(
-            raw_out.at[tick, level, d],
+            raw_part(tick, level, d),
             raw_in.at[tick, level, place],
             raw_sems,
             (tick, level, d),
@@ -1056,7 +1063,7 @@
 
     def own_raw(tick, level):
         return pltpu.make_async_copy(
-            raw_out.at[tick, level, slab],
+            raw_part(tick, level, slab),
             raw_in.at[tick, level, place],
             own_raw_sems.at[tick, level],
         )
@@ -1064,7 +1071,7 @@
     def raw_arrival(tick, level, f):
         source = worker(home if tick == 0 else section, f)
         copy = remote(
-            raw_out.at[tick, level, f],
+            raw_part(tick, level, f),
             raw_in.at[tick, level, f],
             raw_sems,
             (tick, level, f),
@@ -1074,12 +1081,9 @@
 
     def send_raw(tick, level):
         for d in range(lateral):
-            for g in range(groups):
-                for j, x in enumerate(gather_back(raw.at[tick, level], d, g)):
-                    raw_out[(tick, level, d) + tile(g, j)] = x
             copy, foreign = raw_copy(tick, level, d)
             pl.when(foreign)(copy.start)
-            pl.when(jnp.logical_not(foreign))(own_raw(tick, level).start)
+        pl.when((slab_home == tick))(own_raw(tick, level).start)
 
     def wave_back(which, d):
         to = owner(chain + which, d)
@@ -1170,18 +1174,20 @@
                     foreign, own = foreign & is_deep, own & is_deep
                 pl.when(foreign)(copy.wait_recv)
                 pl.when(own)(own_raw(tick, level).wait)
-        total = jnp.zeros((SUB, LANES), jnp.float32)
-        for g in range(groups):
-            for j in range(SUB):
-                value = second = None
-                for f in range(lateral):
-                    a, b = (raw_in[(t, level, f) + tile(g, j)] for t in range(TICKS))
-                    value = a if value is None else value + a
-                    second = b if second is None else second + b
-                value = value + jnp.where(is_deep, second, 0.0)
-                image_ref[(level,) + tile(g, j)] = value
-                total = total + value * value
-        sum_own[pl.ds(level * SUB, SUB), :] = total
+        total = jnp.zeros((groups, LANES), jnp.float32)
+        for i in range(SUB * SUB):
+            value = second = None
+            for f in range(lateral):
+                a, b = (raw_in[t, level, f, i] for t in range(TICKS))
+                value = a if value is None else value + a
+                second = b if second is None else second + b
+            value = value + jnp.where(is_deep, second, 0.0)
+            summed[level, pl.ds(i * groups, groups), :] = value
+            total = total + value * value
+        sum_own[pl.ds(level * SUB, groups), :] = total
+        sum_own[pl.ds(level * SUB + groups, SUB - groups), :] = jnp.zeros(
+            (SUB - groups, LANES), jnp.float32
+        )
 
     def sum_copy(x):
         mate = lax.rem(slab + x, lateral)
@@ -1210,6 +1216,14 @@
             for tick in range(TICKS):
                 copy, foreign = raw_copy(tick, level, n)
                 pl.when(foreign if tick == 0 else foreign & has_next)(copy.wait_send)
+    for level in range(LEVELS):
+        for g in range(groups):
+            part = [
+                summed[level, pl.ds(m * SUB * groups + g, SUB, stride=groups), :]
+                for m in range(SUB)
+            ]
+            for j, x in enumerate(transposed(part)):
+                image_ref[(level,) + tile(g, j)] = x
     total = sum_own[...]
     for x in range(1, lateral):
         sum_copy(x).wait_recv()
@@ -1287,10 +1301,10 @@
             pltpu.VMEM((lateral, 2, length, across), f32),
             pltpu.VMEM((TICKS, lateral, LEVELS, length, across), jnp.int32),
             pltpu.VMEM((tall, LANES), jnp.int32),
-            pltpu.VMEM((TICKS, LEVELS, tall, LANES), f32),
+            pltpu.VMEM((TICKS, LEVELS, SUB * SUB, SUB, LANES), f32),
             pltpu.VMEM((2, lateral, 2, length, across), f32),
-            pltpu.VMEM((TICKS, LEVELS, lateral, length, across), f32),
-            pltpu.VMEM((TICKS, LEVELS, lateral, length, across), f32),
+            pltpu.VMEM((LEVELS, SUB * SUB * length // SUB, LANES), f32),
+            pltpu.VMEM((TICKS, LEVELS, lateral, SUB * SUB, length // SUB, LANES), f32),
             pltpu.VMEM((LEVELS * SUB, LANES), f32),
             pltpu.VMEM((lateral, LEVELS * SUB, LANES), f32),
             pltpu.SemaphoreType.DMA((4,)),

time: 50.6 us -> 49.5 us (0.978); the launches traced: 50.5 us -> 48.6 us
  Pallas kernels: 48.4 us -> 46.6 us
    pallas_call x1, Pallas kernels: 48.4 us -> 46.6 us  [chains(): pl.pallas_call(functools.partial(chain_kernel, count), out_shape=(jax.Sha...]
where the time goes in v6:
time: 49.5 us; the launch traced here: 48.6 us
  Pallas kernels  46.6 us (94%)
  local copies, waits for them, and re-layouts  1.45 us (3%)
  between operations  0.64 us (1%)
    pallas_call x1, Pallas kernels, chains(): pl.pallas_call(functools.partial(chain_kernel, count), out_shape=(jax.Sha...  46.6 us
    unnamed x2, local copies, waits for them, and re-layouts  1.45 us

profile of v6, /device:TPU:1, one launch (start us, length us, event | category | flops | bytes accessed | tf_op | source)
XLA Modules:
  0.0 48.6 jit_solution(3650231729317857765)
XLA Ops:
  0.6 46.6 %shard_map.77 = (f32[2,16,1024]{2,1,0:T(8,128)S(1)}, f32[4,2,16,1024]{3,2,1,0:T(8,128)S(1)}) custom-call(s32[4,4]{1,0:T(4,128)} %entry_ref.1, f32[16]{0:T(128)} %pulsation_ref.1, f32[1,16]{1,0:T(1,128)} %bitcast.3, f32[16,13,2,16]{3,2,1,0:T(2,128)} %bitcast.2, f32[4,2,16,1024]{3,2,1,0:T(8,128)} %wave_ref.1, s32[2,16,1024]{2,1,0:T(8,128)} %map_ref.1), custom_call_target="tpu_custom_call" | custom-call | tf_op jit(solution)/shard_map/pallas_call | solution.py:1278
  47.2 0.7 %copy.10 = f32[2,16,1024]{2,1,0:T(8,128)} copy(f32[2,16,1024]{2,1,0:T(8,128)S(1)} %get-tuple-element.4) | data formatting | bytes 262144
  47.9 0.8 %copy.11 = f32[4,2,16,1024]{3,2,1,0:T(8,128)} copy(f32[4,2,16,1024]{3,2,1,0:T(8,128)S(1)} %get-tuple-element.5) | data formatting | bytes 1048576

commit v7 on v6

--- a/solution.py
+++ b/solution.py
@@ -711,11 +711,12 @@
     on_sems,
     map_sems,
     relay_sems,
-    fin_sems,
-    raw_sems,
+    back_sent,
+    back_got,
+    raw_sent,
+    raw_got,
     sum_sems,
     own_sems,
-    own_raw_sems,
 ):
     length = wave_ref.shape[2]
     groups = length // SUB
@@ -1051,33 +1052,28 @@
 
     def raw_copy(tick, level, d):
         to = owner(chain + tick, d)
-        copy = remote(
-            raw_part(tick, level, d),
-            raw_in.at[tick, level, place],
-            raw_sems,
-            (tick, level, d),
-            device(to),
-            (tick, level, place),
+        copy = pltpu.make_async_remote_copy(
+            src_ref=raw_part(tick, level, d),
+            dst_ref=raw_in.at[tick, level, place],
+            send_sem=raw_sent.at[tick, level],
+            recv_sem=raw_got.at[tick, level],
+            device_id=device(to),
+            device_id_type=MESH,
         )
         return copy, to != me
 
     def own_raw(tick, level):
         return pltpu.make_async_copy(
-            raw_part(tick, level, slab),
-            raw_in.at[tick, level, place],
-            own_raw_sems.at[tick, level],
-        )
-
-    def raw_arrival(tick, level, f):
-        source = worker(home if tick == 0 else section, f)
-        copy = remote(
-            raw_part(tick, level, f),
-            raw_in.at[tick, level, f],
-            raw_sems,
-            (tick, level, f),
-            device(source),
-        )
-        return copy, source != me
+            raw_part(tick, level, slab), raw_in.at[tick, level, place], raw_got.at[tick, level]
+        )
+
+    def raw_arrivals(tick, level):
+        every = raw_in.at[tick, level]
+        return pltpu.make_async_copy(every, every, raw_got.at[tick, level])
+
+    def raw_departures(tick, level, n):
+        some = raw.at[tick, level, :, pl.ds(0, groups * n), :]
+        return pltpu.make_async_copy(some, some, raw_sent.at[tick, level])
 
     def send_raw(tick, level):
         for d in range(lateral):
@@ -1087,30 +1083,21 @@
 
     def wave_back(which, d):
         to = owner(chain + which, d)
-        copy = remote(
-            wave_out.at[which, d],
-            handed_ref.at[place],
-            fin_sems,
-            (which, d),
-            device(to),
-            (1, place),
+        copy = pltpu.make_async_remote_copy(
+            src_ref=wave_out.at[which, d],
+            dst_ref=handed_ref.at[place],
+            send_sem=back_sent.at[which, d],
+            recv_sem=back_got,
+            device_id=device(to),
+            device_id_type=MESH,
         )
         return copy, to != me
 
     def own_back(which):
-        return pltpu.make_async_copy(
-            wave_out.at[which, slab], handed_ref.at[place], own_sems.at[0]
-        )
-
-    def handed_arrival(f):
-        source = worker(jnp.maximum(section, 1), f)
-        copy = remote(
-            wave_out.at[1, f], handed_ref.at[f], fin_sems, (1, f), device(source)
-        )
-        return copy, source != me
+        return pltpu.make_async_copy(wave_out.at[which, slab], handed_ref.at[place], back_got)
 
     def send_wave(which, source):
-        for d in range(lateral):
+        for d in (2, 0, 3, 1):
             for c in range(2):
                 for g in range(groups):
                     for j, x in enumerate(gather_back(source.at[c], d, g)):
@@ -1167,13 +1154,11 @@
 
     for level in range(LEVELS):
         for tick in range(TICKS):
-            for f in range(lateral):
-                copy, foreign = raw_arrival(tick, level, f)
-                own = jnp.logical_not(foreign)
-                if tick == 1:
-                    foreign, own = foreign & is_deep, own & is_deep
-                pl.when(foreign)(copy.wait_recv)
-                pl.when(own)(own_raw(tick, level).wait)
+            arrivals = raw_arrivals(tick, level)
+            if tick == 0:
+                arrivals.wait()
+            else:
+                pl.when(is_deep)(arrivals.wait)
         total = jnp.zeros((groups, LANES), jnp.float32)
         for i in range(SUB * SUB):
             value = second = None
@@ -1191,7 +1176,9 @@
 
     def sum_copy(x):
         mate = lax.rem(slab + x, lateral)
-        return remote(sum_own, sum_in.at[x], sum_sems, (x,), device(owner(section, mate)))
+        return remote(
+            sum_own, sum_in.at[x], sum_sems, (x - 1,), device(owner(section, mate))
+        )
 
     for x in range(1, lateral):
         sum_copy(x).start()
@@ -1212,10 +1199,12 @@
         for which, live in ((0, chain == 0), (1, has_next)):
             copy, foreign = wave_back(which, n)
             pl.when(foreign & live)(copy.wait_send)
-        for level in range(LEVELS):
-            for tick in range(TICKS):
-                copy, foreign = raw_copy(tick, level, n)
-                pl.when(foreign if tick == 0 else foreign & has_next)(copy.wait_send)
+    for level in range(LEVELS):
+        for tick in range(TICKS):
+            live = True if tick == 0 else has_next
+            own = side == tick
+            pl.when(own & live)(raw_departures(tick, level, lateral - 1).wait)
+            pl.when(jnp.logical_not(own) & live)(raw_departures(tick, level, lateral).wait)
     for level in range(LEVELS):
         for g in range(groups):
             part = [
@@ -1238,10 +1227,7 @@
             for j in range(SUB):
                 where = (level,) + tile(g, j)
                 image_ref[where] = image_ref[where] * scale
-    for f in range(lateral):
-        copy, foreign = handed_arrival(f)
-        pl.when(foreign)(copy.wait_recv)
-        pl.when(jnp.logical_not(foreign))(own_back(0).wait)
+    pltpu.make_async_copy(handed_ref, handed_ref, back_got).wait()
     for x in range(1, lateral):
         sum_copy(x).wait_send()
 
@@ -1313,11 +1299,12 @@
             dma(lateral),
             dma(TICKS, 2),
             dma(TICKS, 2),
-            dma(2, lateral),
-            dma(TICKS, LEVELS, lateral),
-            dma(lateral),
+            pltpu.SemaphoreType.DMA((2, lateral)),
+            pltpu.SemaphoreType.DMA,
+            pltpu.SemaphoreType.DMA((TICKS, LEVELS)),
+            pltpu.SemaphoreType.DMA((TICKS, LEVELS)),
+            dma(lateral - 1),
             pltpu.SemaphoreType.DMA((2,)),
-            pltpu.SemaphoreType.DMA((TICKS, LEVELS)),
         ],
         compiler_params=pltpu.CompilerParams(
             collective_id=0, has_side_effects=True, vmem_limit_bytes=32 * 1024 * 1024

time: 49.5 us -> 49.2 us (level)
  no operation moved by 1% of the time
where the time goes in v7:
time: 49.2 us; the launch traced here: 48.3 us
  Pallas kernels  46.2 us (94%)
  local copies, waits for them, and re-layouts  1.45 us (3%)
  between operations  0.64 us (1%)
    pallas_call x1, Pallas kernels, chains(): pl.pallas_call(functools.partial(chain_kernel, count), out_shape=(jax.Sha...  46.2 us
    unnamed x2, local copies, waits for them, and re-layouts  1.45 us

profile of v7, /device:TPU:1, one launch (start us, length us, event | category | flops | bytes accessed | tf_op | source)
XLA Modules:
  0.0 48.3 jit_solution(8887012520791121166)
XLA Ops:
  0.6 46.2 %shard_map.77 = (f32[2,16,1024]{2,1,0:T(8,128)S(1)}, f32[4,2,16,1024]{3,2,1,0:T(8,128)S(1)}) custom-call(s32[4,4]{1,0:T(4,128)} %entry_ref.1, f32[16]{0:T(128)} %pulsation_ref.1, f32[1,16]{1,0:T(1,128)} %bitcast.3, f32[16,13,2,16]{3,2,1,0:T(2,128)} %bitcast.2, f32[4,2,16,1024]{3,2,1,0:T(8,128)} %wave_ref.1, s32[2,16,1024]{2,1,0:T(8,128)} %map_ref.1), custom_call_target="tpu_custom_call" | custom-call | tf_op jit(solution)/shard_map/pallas_call | solution.py:1264
  46.9 0.7 %copy.10 = f32[2,16,1024]{2,1,0:T(8,128)} copy(f32[2,16,1024]{2,1,0:T(8,128)S(1)} %get-tuple-element.4) | data formatting | bytes 262144
  47.5 0.8 %copy.11 = f32[4,2,16,1024]{3,2,1,0:T(8,128)} copy(f32[4,2,16,1024]{3,2,1,0:T(8,128)S(1)} %get-tuple-element.5) | data formatting | bytes 1048576

commit v8 on v7

--- a/solution.py
+++ b/solution.py
@@ -732,7 +732,6 @@
     slab = lax.rem(place + half, lateral)
     home = lax.rem(section + 1, SECTIONS)
     near = side == 0
-    slab_home = side
     has_next = chain < SECTIONS - 1
     is_deep = section > 0
 
@@ -1079,7 +1078,7 @@
         for d in range(lateral):
             copy, foreign = raw_copy(tick, level, d)
             pl.when(foreign)(copy.start)
-        pl.when((slab_home == tick))(own_raw(tick, level).start)
+        pl.when(side == tick)(own_raw(tick, level).start)
 
     def wave_back(which, d):
         to = owner(chain + which, d)
@@ -1105,6 +1104,37 @@
             copy, foreign = wave_back(which, d)
             pl.when(foreign)(copy.start)
             pl.when(jnp.logical_not(foreign))(own_back(which).start)
+
+    def sum_copy(x):
+        mate = lax.rem(slab + x, lateral)
+        return remote(
+            sum_own, sum_in.at[x], sum_sems, (x - 1,), device(owner(section, mate))
+        )
+
+    def square_up():
+        for level in range(LEVELS):
+            for tick in range(TICKS):
+                arrivals = raw_arrivals(tick, level)
+                if tick == 0:
+                    arrivals.wait()
+                else:
+                    pl.when(is_deep)(arrivals.wait)
+            total = jnp.zeros((groups, LANES), jnp.float32)
+            for i in range(SUB * SUB):
+                value = second = None
+                for f in range(lateral):
+                    a, b = (raw_in[t, level, f, i] for t in range(TICKS))
+                    value = a if value is None else value + a
+                    second = b if second is None else second + b
+                value = value + jnp.where(is_deep, second, 0.0)
+                summed[level, pl.ds(i * groups, groups), :] = value
+                total = total + value * value
+            sum_own[pl.ds(level * SUB, groups), :] = total
+            sum_own[pl.ds(level * SUB + groups, SUB - groups), :] = jnp.zeros(
+                (SUB - groups, LANES), jnp.float32
+            )
+        for x in range(1, lateral):
+            sum_copy(x).start()
 
     pass_map_on(0)
     for h in range(2):
@@ -1148,40 +1178,12 @@
         fill(1, 1)
         unit(1, 0, starts.at[3])
         send_raw(1, 0)
+        pl.when(jnp.logical_not(is_deep))(square_up)
         unit(1, 1, last)
         send_raw(1, 1)
         send_wave(1, last)
 
-    for level in range(LEVELS):
-        for tick in range(TICKS):
-            arrivals = raw_arrivals(tick, level)
-            if tick == 0:
-                arrivals.wait()
-            else:
-                pl.when(is_deep)(arrivals.wait)
-        total = jnp.zeros((groups, LANES), jnp.float32)
-        for i in range(SUB * SUB):
-            value = second = None
-            for f in range(lateral):
-                a, b = (raw_in[t, level, f, i] for t in range(TICKS))
-                value = a if value is None else value + a
-                second = b if second is None else second + b
-            value = value + jnp.where(is_deep, second, 0.0)
-            summed[level, pl.ds(i * groups, groups), :] = value
-            total = total + value * value
-        sum_own[pl.ds(level * SUB, groups), :] = total
-        sum_own[pl.ds(level * SUB + groups, SUB - groups), :] = jnp.zeros(
-            (SUB - groups, LANES), jnp.float32
-        )
-
-    def sum_copy(x):
-        mate = lax.rem(slab + x, lateral)
-        return remote(
-            sum_own, sum_in.at[x], sum_sems, (x - 1,), device(owner(section, mate))
-        )
-
-    for x in range(1, lateral):
-        sum_copy(x).start()
+    pl.when(is_deep | jnp.logical_not(has_next))(square_up)
     for tick in range(TICKS):
         for y in range(2):
             copy, live = map_copy(tick, y)

time: 49.2 us -> 49.2 us (level)
  no operation moved by 1% of the time
where the time goes in v8:
time: 49.2 us; the launch traced here: 48.3 us
  Pallas kernels  46.2 us (94%)
  local copies, waits for them, and re-layouts  1.45 us (3%)
  between operations  0.64 us (1%)
    pallas_call x1, Pallas kernels, chains(): pl.pallas_call(functools.partial(chain_kernel, count), out_shape=(jax.Sha...  46.2 us
    unnamed x2, local copies, waits for them, and re-layouts  1.45 us

profile of v8, /device:TPU:1, one launch (start us, length us, event | category | flops | bytes accessed | tf_op | source)
XLA Modules:
  0.0 48.3 jit_solution(9118288258133273203)
XLA Ops:
  0.6 46.2 %shard_map.77 = (f32[2,16,1024]{2,1,0:T(8,128)S(1)}, f32[4,2,16,1024]{3,2,1,0:T(8,128)S(1)}) custom-call(s32[4,4]{1,0:T(4,128)} %entry_ref.1, f32[16]{0:T(128)} %pulsation_ref.1, f32[1,16]{1,0:T(1,128)} %bitcast.3, f32[16,13,2,16]{3,2,1,0:T(2,128)} %bitcast.2, f32[4,2,16,1024]{3,2,1,0:T(8,128)} %wave_ref.1, s32[2,16,1024]{2,1,0:T(8,128)} %map_ref.1), custom_call_target="tpu_custom_call" | custom-call | tf_op jit(solution)/shard_map/pallas_call | solution.py:1266
  46.9 0.7 %copy.10 = f32[2,16,1024]{2,1,0:T(8,128)} copy(f32[2,16,1024]{2,1,0:T(8,128)S(1)} %get-tuple-element.4) | data formatting | bytes 262144
  47.5 0.8 %copy.11 = f32[4,2,16,1024]{3,2,1,0:T(8,128)} copy(f32[4,2,16,1024]{3,2,1,0:T(8,128)S(1)} %get-tuple-element.5) | data formatting | bytes 1048576
